TPU v7x, 32 devices: a whole 2x2x4 slice. The times are simulated.
32 devices in a mesh: seq: 16 (over z, x, core), tp: 2 (over y).
Axes of the slice: x: 2, y: 2, z: 4, core: 2. Of those that a mesh axis runs over, the one named last changes fastest.
Arguments:
- tokens: bfloat16 [4096, 4096], P('seq', 'tp'), may hold values from -6 to 6
- decay_rate: float32 [4096, 16], P('tp'), as said below
- angle: float32 [4096, 16], P('tp'), may hold values from -3.140625 to 3.140625
- in_coef: float32 [4096, 16], P('tp'), may hold values from -4 to 4
- out_coef: float32 [2, 4096, 16], P(None, 'tp'), may hold values from -1.5 to 1.5
- skip_coef: float32 [4096], P('tp'), may hold values from 0.3 to 1.5
- gate_weight: bfloat16 [4096, 4096], P('seq', 'tp'), may hold values from -0.09375 to 0.09375
- out_weight: bfloat16 [4096, 4096], P('seq', 'tp'), may hold values from -0.09375 to 0.09375
Outputs:
- mixed_out: bfloat16 [4096, 4096], P('seq', 'tp')
Inputs may be any that keep to these rules, and one draw needn't show every extreme that they name: `decay_rate`: every entry is positive and below 0.034.
All inputs are finite; a program needn't handle non-finite values.
Results may differ from a plain program's by a relative error of at most 0.01.
Values may be sent and summed in bfloat16 or wider, within the bound.
A program may use at most 192 MiB of HBM per device.

v0:
```python
import jax
import jax.numpy as jnp
from jax import lax
from jax.experimental import pallas as pl
from jax.experimental.pallas import tpu as pltpu
from jax.sharding import PartitionSpec as P

LANES = 128
UNROLL = 8
PIECE_BYTES = 512 * 1024


def small_gather(array, name, axis, split_axis):
    count = lax.axis_size(name)
    total = array.size * array.dtype.itemsize * count
    pieces = max(1, total // PIECE_BYTES)
    while array.shape[split_axis] % pieces:
        pieces -= 1
    parts = jnp.split(array, pieces, axis=split_axis)
    done = [lax.all_gather(part, name, axis=axis, tiled=True) for part in parts]
    return done[0] if pieces == 1 else jnp.concatenate(done, axis=split_axis)


def step_state(state, values, q_re, q_im):
    advanced = []
    for (re, im), a, b in zip(state, q_re, q_im):
        advanced.append((a * re - b * im + values, a * im + b * re))
    return advanced


def end_kernel(x_ref, q_re_ref, q_im_ref, end_re_ref, end_im_ref):
    dims = q_re_ref.shape[0]
    q_re = [q_re_ref[h] for h in range(dims)]
    q_im = [q_im_ref[h] for h in range(dims)]
    zero = jnp.zeros(q_re[0].shape, jnp.float32)

    def body(i, state):
        for u in range(UNROLL):
            state = step_state(state, x_ref[i * UNROLL + u], q_re, q_im)
        return state

    state = lax.fori_loop(0, x_ref.shape[0] // UNROLL, body, [(zero, zero)] * dims)
    for h in range(dims):
        end_re_ref[h] = state[h][0]
        end_im_ref[h] = state[h][1]


def smooth_kernel(
    position_ref, x_ref, q_re_ref, q_im_ref, c_re_ref, c_im_ref, span_re_ref, span_im_ref,
    ends_re_ref, ends_im_ref, skip_ref, y_ref,
):
    dims = q_re_ref.shape[0]
    zero = jnp.zeros(q_re_ref.shape[1:], jnp.float32)

    def horner(k, state):
        moved = []
        for h in range(dims):
            re, im = state[h]
            a, b = span_re_ref[h], span_im_ref[h]
            moved.append((
                a * re - b * im + ends_re_ref[k, h].astype(jnp.float32),
                a * im + b * re + ends_im_ref[k, h].astype(jnp.float32),
            ))
        return moved

    state = lax.fori_loop(0, position_ref[0], horner, [(zero, zero)] * dims)
    q_re = [q_re_ref[h] for h in range(dims)]
    q_im = [q_im_ref[h] for h in range(dims)]
    c_re = [c_re_ref[h] for h in range(dims)]
    c_im = [c_im_ref[h] for h in range(dims)]

    @pl.when(pl.program_id(1) == 0)
    def _():
        y_ref[...] = x_ref[...] * skip_ref[...][None]

    def body(i, state):
        for u in range(UNROLL):
            t = i * UNROLL + u
            state = step_state(state, x_ref[t], q_re, q_im)
            sums = [c_re[h] * state[h][0] - c_im[h] * state[h][1] for h in range(dims)]
            while len(sums) > 1:
                sums = [sum(sums[k:k + 2]) for k in range(0, len(sums), 2)]
            y_ref[t] += sums[0]
        return state

    lax.fori_loop(0, x_ref.shape[0] // UNROLL, body, state)


def per_device(tokens, decay_rate, angle, in_coef, out_coef, skip_coef, gate_weight, out_weight):
    rows, channels = tokens.shape
    dims = decay_rate.shape[1]
    tiles = channels // LANES
    sub = 8 if tiles % 8 == 0 else tiles
    half = dims // 2 if dims % 2 == 0 else dims
    grid = (tiles // sub, dims // half)

    gate_all = lax.all_gather(gate_weight, "seq", axis=0, tiled=True)
    out_all = lax.all_gather(out_weight, "seq", axis=0, tiled=True)

    def spread(table):
        return table.T.reshape(dims, tiles, LANES)

    rate = spread(decay_rate)
    theta = spread(angle)
    magnitude = 1.0 - rate
    scaled = spread(in_coef) * jnp.sqrt(1.0 - magnitude * magnitude)
    c_re = scaled * spread(out_coef[0])
    c_im = scaled * spread(out_coef[1])
    q_re = magnitude * jnp.cos(theta)
    q_im = magnitude * jnp.sin(theta)
    span_mag = jnp.exp(rows * jnp.log1p(-rate))
    span_re = span_mag * jnp.cos(rows * theta)
    span_im = span_mag * jnp.sin(rows * theta)
    values = tokens.astype(jnp.float32).reshape(rows, tiles, LANES)

    x_spec = pl.BlockSpec((rows, sub, LANES), lambda g, h: (0, g, 0))
    table_spec = pl.BlockSpec((half, sub, LANES), lambda g, h: (h, g, 0))
    table_shape = jax.ShapeDtypeStruct((dims, tiles, LANES), jnp.float32)
    end_re, end_im = pl.pallas_call(
        end_kernel,
        grid=grid,
        in_specs=[x_spec, table_spec, table_spec],
        out_specs=[table_spec, table_spec],
        out_shape=[table_shape, table_shape],
        name="end_state",
    )(values, q_re, q_im)

    columns = small_gather(tokens, "tp", 1, 0)
    ends_re = small_gather(end_re.astype(jnp.bfloat16)[None], "seq", 0, 1)
    ends_im = small_gather(end_im.astype(jnp.bfloat16)[None], "seq", 0, 1)
    devices = ends_re.shape[0]
    ends_spec = pl.BlockSpec((devices, half, sub, LANES), lambda g, h: (0, h, g, 0))
    position = lax.axis_index("seq").astype(jnp.int32).reshape(1)
    smoothed = pl.pallas_call(
        smooth_kernel,
        grid=grid,
        in_specs=[pl.BlockSpec(memory_space=pltpu.SMEM), x_spec]
        + [table_spec] * 6
        + [ends_spec, ends_spec, pl.BlockSpec((sub, LANES), lambda g, h: (g, 0))],
        out_specs=x_spec,
        out_shape=jax.ShapeDtypeStruct((rows, tiles, LANES), jnp.float32),
        name="smooth",
    )(
        position, values, q_re, q_im, c_re, c_im, span_re, span_im, ends_re, ends_im,
        skip_coef.reshape(tiles, LANES),
    ).reshape(rows, channels)
    activated = jax.nn.silu(smoothed)
    gate_pre = jnp.dot(columns, gate_all, preferred_element_type=jnp.float32)
    hidden = (activated * jax.nn.sigmoid(gate_pre)).astype(jnp.bfloat16)
    hidden_all = small_gather(hidden, "tp", 1, 0)
    mixed_out = jnp.dot(hidden_all, out_all, preferred_element_type=jnp.float32)
    return mixed_out.astype(jnp.bfloat16)


def solution(mesh):
    in_specs = (
        P("seq", "tp"),
        P("tp", None),
        P("tp", None),
        P("tp", None),
        P(None, "tp", None),
        P("tp"),
        P("seq", "tp"),
        P("seq", "tp"),
    )
    return jax.shard_map(
        per_device, mesh=mesh, in_specs=in_specs, out_specs=P("seq", "tp"), check_vma=False
    )
```

profile of v0, /device:TPU:0, one launch (start us, length us, event | category | flops | bytes accessed | tf_op | source)
XLA Modules:
  0.0 295.9 jit_solution(1825525083746880362)
XLA Ops:
  6.6 0.7 all-gather.3.cloned.1.call-update
  7.3 0.7 all-gather.5.cloned.1.call-update
  8.1 1.1 multiply_bitcast_fusion
  10.8 1.7 copy.9
  15.1 10.0 %end_state.1 = (f32[16,16,128]{2,1,0:T(8,128)}, f32[16,16,128]{2,1,0:T(8,128)}) custom-call(f32[256,16,128]{2,1,0:T(8,128)} %bitcast.57, f32[16,16,128]{2,1,0:T(8,128)} %bitcast.60, f32[16,16,128]{2,1,0:T(8,128)} %bitcast.62), custom_call_target="tpu_custom_call" | custom-call | tf_op jit(solution)/shard_map/end_state/pallas_call | solution.py:119
  25.1 1.0 convert_bitcast_fusion.1
  26.1 27.9 %all_gather.44 = bf16[16,8,16,128]{3,2,1,0:T(8,128)(2,1)S(1)} all-gather(bf16[1,8,16,128]{3,2,1,0:T(8,128)(2,1)S(1)} %get-tuple-element.25), channel_id=1, replica_groups=mesh['seq'=16,'tp'=2] {'seq'}, dimensions={0}, use_global_device_ids=true | all-gather | bytes 557056 | tf_op jit(solution)/shard_map/all_gather | solution.py:20
  54.0 20.6 %all_gather.45 = bf16[16,8,16,128]{3,2,1,0:T(8,128)(2,1)S(1)} all-gather(bf16[1,8,16,128]{3,2,1,0:T(8,128)(2,1)S(1)} %get-tuple-element.26), channel_id=1, replica_groups=mesh['seq'=16,'tp'=2] {'seq'}, dimensions={0}, use_global_device_ids=true | all-gather | bytes 557056 | tf_op jit(solution)/shard_map/all_gather | solution.py:20
  74.6 1.1 pad_maximum_fusion.1.ends_im_ref
  75.7 24.5 %all_gather.42 = bf16[16,8,16,128]{3,2,1,0:T(8,128)(2,1)S(1)} all-gather(bf16[1,8,16,128]{3,2,1,0:T(8,128)(2,1)S(1)} %get-tuple-element.27), channel_id=1, replica_groups=mesh['seq'=16,'tp'=2] {'seq'}, dimensions={0}, use_global_device_ids=true | all-gather | bytes 557056 | tf_op jit(solution)/shard_map/all_gather | solution.py:20
  100.2 21.8 %all_gather.43 = bf16[16,8,16,128]{3,2,1,0:T(8,128)(2,1)S(1)} all-gather(bf16[1,8,16,128]{3,2,1,0:T(8,128)(2,1)S(1)} %get-tuple-element.28), channel_id=1, replica_groups=mesh['seq'=16,'tp'=2] {'seq'}, dimensions={0}, use_global_device_ids=true | all-gather | bytes 557056 | tf_op jit(solution)/shard_map/all_gather | solution.py:20
  122.1 1.1 pad_maximum_fusion.ends_re_ref
  123.2 15.4 %smooth.1 = f32[256,16,128]{2,1,0:T(8,128)} custom-call(s32[1]{0:T(128)} %bitcast.position_ref, f32[256,16,128]{2,1,0:T(8,128)} %bitcast.58, f32[16,16,128]{2,1,0:T(8,128)} %bitcast.61, f32[16,16,128]{2,1,0:T(8,128)} %bitcast.63, f32[16,16,128]{2,1,0:T(8,128)} %bitcast.64, f32[16,16,128]{2,1,0:T(8,128)} %bitcast.65, f32[16,16,128]{2,1,0:T(8,128)} %bitcast.66, ...), custom_call_target="tpu_custom_call" | custom-call | tf_op jit(solution)/shard_map/smooth/pallas_call | solution.py:134
  138.7 9.4 %all_gather.46 = bf16[64,4096]{1,0:T(8,128)(2,1)S(1)} all-gather(bf16[64,2048]{1,0:T(8,128)(2,1)S(1)} %get-tuple-element.13), channel_id=1, replica_groups=mesh['seq'=16,'tp'=2] {'tp'}, dimensions={1}, use_global_device_ids=true | all-gather | bytes 786432 | tf_op jit(solution)/shard_map/all_gather | solution.py:20
  148.1 8.5 %all_gather.47 = bf16[64,4096]{1,0:T(8,128)(2,1)S(1)} all-gather(bf16[64,2048]{1,0:T(8,128)(2,1)S(1)} %get-tuple-element.14), channel_id=1, replica_groups=mesh['seq'=16,'tp'=2] {'tp'}, dimensions={1}, use_global_device_ids=true | all-gather | bytes 786432 | tf_op jit(solution)/shard_map/all_gather | solution.py:20
  156.6 7.8 %all_gather.48 = bf16[64,4096]{1,0:T(8,128)(2,1)} all-gather(bf16[64,2048]{1,0:T(8,128)(2,1)S(1)} %get-tuple-element.16), channel_id=1, replica_groups=mesh['seq'=16,'tp'=2] {'tp'}, dimensions={1}, use_global_device_ids=true | all-gather | bytes 786432 | tf_op jit(solution)/shard_map/all_gather | solution.py:20
  164.3 7.1 %all_gather.49 = bf16[64,4096]{1,0:T(8,128)(2,1)} all-gather(bf16[64,2048]{1,0:T(8,128)(2,1)S(1)} %get-tuple-element.15), channel_id=1, replica_groups=mesh['seq'=16,'tp'=2] {'tp'}, dimensions={1}, use_global_device_ids=true | all-gather | bytes 786432 | tf_op jit(solution)/shard_map/all_gather | solution.py:20
  171.5 11.4 %fusion.4 = bf16[256,2048]{1,0:T(8,128)(2,1)S(1)} fusion(bf16[4096,2048]{1,0:T(8,128)(2,1)} %all-gather.3.cloned.1.call-done, f32[32,8,16,128]{3,2,1,0:T(8,128)S(1)} %bitcast.59, bf16[64,4096]{1,0:T(8,128)(2,1)} %all_gather.49, bf16[64,4096]{1,0:T(8,128)(2,1)} %all_gather.48, bf16[64,4096]{1,0:T(8,128)(2,1)S(1)} %all_gather.47, ...), kind=kOutput, calls=%fused_computation.5 | convolution fusion | flops 4308074496 | bytes 22020096 | tf_op jit(solution)/shard_map/dot_general | solution.py:148
  183.0 7.5 %all_gather.51 = bf16[64,4096]{1,0:T(8,128)(2,1)S(1)} all-gather(bf16[64,2048]{1,0:T(8,128)(2,1)S(1)} %get-tuple-element.9), channel_id=1, replica_groups=mesh['seq'=16,'tp'=2] {'tp'}, dimensions={1}, use_global_device_ids=true | all-gather | bytes 786432 | tf_op jit(solution)/shard_map/all_gather | solution.py:20
  190.4 8.2 %all_gather.52 = bf16[64,4096]{1,0:T(8,128)(2,1)S(1)} all-gather(bf16[64,2048]{1,0:T(8,128)(2,1)S(1)} %get-tuple-element.12), channel_id=1, replica_groups=mesh['seq'=16,'tp'=2] {'tp'}, dimensions={1}, use_global_device_ids=true | all-gather | bytes 786432 | tf_op jit(solution)/shard_map/all_gather | solution.py:20
  198.7 9.2 %all_gather.53 = bf16[64,4096]{1,0:T(8,128)(2,1)S(1)} all-gather(bf16[64,2048]{1,0:T(8,128)(2,1)S(1)} %get-tuple-element.11), channel_id=1, replica_groups=mesh['seq'=16,'tp'=2] {'tp'}, dimensions={1}, use_global_device_ids=true | all-gather | bytes 786432 | tf_op jit(solution)/shard_map/all_gather | solution.py:20
  207.8 7.0 %all_gather.54 = bf16[64,4096]{1,0:T(8,128)(2,1)S(1)} all-gather(bf16[64,2048]{1,0:T(8,128)(2,1)S(1)} %get-tuple-element.10), channel_id=1, replica_groups=mesh['seq'=16,'tp'=2] {'tp'}, dimensions={1}, use_global_device_ids=true | all-gather | bytes 786432 | tf_op jit(solution)/shard_map/all_gather | solution.py:20
  214.9 65.0 %all-gather.5.cloned.1.call-done = bf16[4096,2048]{1,0:T(8,128)(2,1)} async-done(((bf16[256,2048]{1,0:T(8,128)(2,1)}), bf16[4096,2048]{1,0:T(8,128)(2,1)}) %all-gather.5.cloned.1.call-update) | async-done | bytes 16777232 | tf_op jit(solution)/shard_map/all_gather | solution.py:98
  279.8 9.2 %convolution_convert_fusion = bf16[256,2048]{1,0:T(8,128)(2,1)} fusion(bf16[4096,2048]{1,0:T(8,128)(2,1)} %all-gather.5.cloned.1.call-done, bf16[64,4096]{1,0:T(8,128)(2,1)S(1)} %all_gather.54, bf16[64,4096]{1,0:T(8,128)(2,1)S(1)} %all_gather.53, bf16[64,4096]{1,0:T(8,128)(2,1)S(1)} %all_gather.52, bf16[64,4096]{1,0:T(8,128)(2,1)S(1)} %all_gather.51), kind=kOutput, calls=%fused_computation.6 | convolution fusion | flops 4303880192 | bytes 19922944 | tf_op jit(solution)/shard_map/dot_general | solution.py:151
  (26 shorter events, 4.5 us)
Async XLA Ops:
  6.5 1.5 copy-start.3
  6.5 1.5 copy-start.5
  6.5 1.5 copy-start.2
  6.5 1.5 copy-start.4
  6.5 4.0 %copy-start = (bf16[256,2048]{1,0:T(8,128)(2,1)S(1)}, bf16[256,2048]{1,0:T(8,128)(2,1)}, u32[]{:S(2)}) copy-start(bf16[256,2048]{1,0:T(8,128)(2,1)} %param.8) | copy-start | bytes 3145732
  6.5 164.9 %all-gather.3.cloned.1.call-start = ((), (), s32[]{:S(2)}) async-start(), calls=%async_computation | async-start | bytes 17825792 | tf_op jit(solution)/shard_map/all_gather | solution.py:97
  7.3 272.6 %all-gather.5.cloned.1.call-start = ((), (), s32[]{:S(2)}) async-start(), calls=%async_computation.1 | async-start | bytes 17825792 | tf_op jit(solution)/shard_map/all_gather | solution.py:98
  138.6 32.8 %copy-start.1 = (f32[256,16,128]{2,1,0:T(8,128)S(1)}, f32[256,16,128]{2,1,0:T(8,128)}, u32[]{:S(2)}) copy-start(f32[256,16,128]{2,1,0:T(8,128)} %smooth.1) | copy-start | bytes 6291460
Sparse Core Ops, SparseCore 0:
  9.5 143.1 all-gather.2
  154.9 124.9 all-gather.4
where the time goes:
time: 296 us
  blocking collectives  160 us (54%)
  waiting for transfers between devices  66.3 us (22%)
  Pallas kernels  25.4 us (9%)
  matrix products  20.6 us (7%)
  between operations  13.5 us (5%)
  local copies, waits for them, and re-layouts  5.88 us (2%)
  other arithmetic  4.47 us (2%)
    all_gather x12, blocking collectives, small_gather(): done = [lax.all_gather(part, name, axis=axis, tiled=True) for part in parts]  160 us
    all_gather x1, waiting for transfers between devices, per_device(): out_all = lax.all_gather(out_weight, 'seq', axis=0, tiled=True)  65 us
    pallas_call x1, Pallas kernels, per_device(): pl.pallas_call(smooth_kernel, grid=grid, in_specs=[pl.BlockSpec(memory_sp...  15.4 us
    dot_general x1, matrix products, per_device(): gate_pre = jnp.dot(columns, gate_all, preferred_element_type=jnp.float32)  11.4 us
    pallas_call x1, Pallas kernels, per_device(): pl.pallas_call(end_kernel, grid=grid, in_specs=[x_spec, table_spec, table...  9.97 us
    dot_general x1, matrix products, per_device(): mixed_out = jnp.dot(hidden_all, out_all, preferred_element_type=jnp.float32)  9.2 us
  transfers between devices with their start and end apart: 2, of which 1 were waited for; matrix products, arithmetic and copies ran while one was open for 7% of the time, Pallas kernels for 9%

commit v1 on v0

v1 whole, which is shorter than its diff:
```python
import functools

import jax
import jax.numpy as jnp
from jax import lax
from jax.experimental import pallas as pl
from jax.experimental.pallas import tpu as pltpu
from jax.sharding import PartitionSpec as P

LANES = 128
UNROLL = 8
MESH = pl.DeviceIdType.MESH
F32, BF16 = jnp.float32, jnp.bfloat16


def mixer_kernel(
    lines, parts, dims,
    tok, gate_w, out_w, q_re_ref, q_im_ref, c_re_ref, c_im_ref, s_re_ref, s_im_ref, skip_ref,
    out_ref,
    te, x2d, y2d, st, cin, cout, A, W, own, cs, cr, hid, ost,
    l_w, l_te, l_a, sw_s, sw_r, te_s, te_r, z_s, z_r, x_s, x_r, p_s, p_r, po_s, ch_s, ch_r, c_s, c_r, o_s, o_r,
):
    rows, width = tok.shape
    bw = gate_w.shape[0]
    blk = 2 * bw
    chunks = width // blk
    halves = chunks // 2
    sub = chunks * bw // LANES
    tiles = bw // LANES
    two = 2 * rows

    s = lax.axis_index("seq")
    y = lax.axis_index("tp")
    z, x, c = s // 4, (s // 2) % 2, s % 2
    pos = z * 2 + x

    def dev(zz, xx, cc, yy):
        return ((zz * 2 + xx) * 2 + cc, yy)

    partner = dev(z, x, 1 - c, y)
    is_mid = (z > 0) & (z < lines - 1)

    def hint(v, m):
        return v if isinstance(v, int) else pl.multiple_of(v, m)

    def ds(start, size, m):
        return pl.ds(hint(start, m), size)

    def remote(src, dst, ssem, rsem, where):
        return pltpu.make_async_remote_copy(src, dst, ssem, rsem, device_id=where, device_id_type=MESH)

    weights = (gate_w, out_w)
    others = [(xx, yy) for yy in range(parts) for xx in range(2)]
    peers = others[1:]

    def w_local(w, j):
        return pltpu.make_async_copy(
            weights[w].at[:, ds(j * blk + c * bw, bw, bw)],
            W.at[w, j, ds(z * blk + c * bw, bw, bw)], l_w.at[w, j])

    def w_swap(w, j):
        return remote(
            weights[w].at[:, ds(j * blk + (1 - c) * bw, bw, bw)],
            W.at[w, j, ds(z * blk + c * bw, bw, bw)], sw_s.at[w, j], sw_r.at[w, j], partner)

    def te_local(j):
        return pltpu.make_async_copy(
            tok.at[:, ds(j * blk + c * bw, bw, bw)], te.at[ds(c * rows, rows, rows), ds(j * bw, bw, bw)], l_te.at[j])

    def te_swap(j):
        return remote(
            tok.at[:, ds(j * blk + (1 - c) * bw, bw, bw)],
            te.at[ds(c * rows, rows, rows), ds(j * bw, bw, bw)], te_s.at[j], te_r.at[j], partner)

    def piece(w, j, o):
        return W.at[w, j, ds(o * blk, blk, blk)]

    def z_send(w, j, o, side):
        where = dev(z + (1 if side else -1), x, c, y)
        return remote(piece(w, j, o), piece(w, j, o), z_s.at[side, w, j, o], z_r.at[w, j, o], where)

    def at_peer(dx, dy):
        return (x + dx) % 2, (y + dy) % parts

    def a_cols(yy, jj):
        return ds((yy * halves + jj) * blk, blk, blk)

    def slot(dx, yy):
        return dx * parts + yy

    def t_send(dx, dy, jj):
        xx, yy = at_peer(dx, dy)
        return remote(
            tok.at[:, ds((2 * jj + xx) * blk, blk, blk)],
            A.at[0, ds((x * 2 + c) * rows, rows, rows), a_cols(y, jj)],
            x_s.at[0, dx * parts + dy, jj], x_r.at[0, slot(dx, y), jj], dev(z, xx, c, yy))

    def t_got(dx, dy, jj):
        xx, yy = at_peer(dx, dy)
        dst = A.at[0, ds((xx * 2 + c) * rows, rows, rows), a_cols(yy, jj)]
        return remote(dst, dst, x_s.at[0, dx * parts + dy, jj], x_r.at[0, slot(dx, yy), jj], dev(z, xx, c, yy))

    def t_local(jj):
        return pltpu.make_async_copy(
            tok.at[:, ds((2 * jj + x) * blk, blk, blk)],
            A.at[0, ds((x * 2 + c) * rows, rows, rows), a_cols(y, jj)], l_a.at[jj])

    def t_own(jj):
        return remote(
            tok.at[:, ds((2 * jj + x) * blk, blk, blk)],
            A.at[0, ds((x * 2 + c) * rows, rows, rows), a_cols(y, jj)],
            p_s.at[0, 0, jj], p_r.at[0, slot(0, y), jj], partner)

    def t_pass(dx, dy, jj):
        xx, yy = at_peer(dx, dy)
        ref = A.at[0, ds((xx * 2 + c) * rows, rows, rows), a_cols(yy, jj)]
        return remote(ref, ref, p_s.at[0, dx * parts + dy, jj], p_r.at[0, slot(dx, yy), jj], partner)

    def t_passed(dx, dy, jj):
        xx, yy = at_peer(dx, dy)
        ref = A.at[0, ds((xx * 2 + 1 - c) * rows, rows, rows), a_cols(yy, jj)]
        return remote(ref, ref, p_s.at[0, dx * parts + dy, jj], p_r.at[0, slot(dx, yy), jj], partner)

    def h_ref(xx, yy, jj, cc):
        cols = ds((yy * halves + jj) * blk + cc * bw, bw, bw)
        return A.at[1, ds(xx * two, two, two), cols]

    def h_send(dx, dy, jj, j):
        xx, yy = at_peer(dx, dy)
        return remote(
            hid.at[j], h_ref(x, y, jj, c), x_s.at[1, dx * parts + dy, jj], x_r.at[1, slot(dx, y), jj],
            dev(z, xx, c, yy))

    def h_got(dx, dy, jj):
        xx, yy = at_peer(dx, dy)
        ref = h_ref(xx, yy, jj, c)
        return remote(ref, ref, x_s.at[1, dx * parts + dy, jj], x_r.at[1, slot(dx, yy), jj], dev(z, xx, c, yy))

    def h_own(jj, j):
        return remote(hid.at[j], h_ref(x, y, jj, c), p_s.at[1, 0, jj], p_r.at[1, slot(0, y), jj], partner)

    def h_pass(dx, dy, jj):
        xx, yy = at_peer(dx, dy)
        ref = h_ref(xx, yy, jj, c)
        return remote(ref, ref, p_s.at[1, dx * parts + dy, jj], p_r.at[1, slot(dx, yy), jj], partner)

    def h_passed(dx, dy, jj):
        xx, yy = at_peer(dx, dy)
        ref = h_ref(xx, yy, jj, 1 - c)
        return remote(ref, ref, p_s.at[1, dx * parts + dy, jj], p_r.at[1, slot(dx, yy), jj], partner)

    def c_send(w, j):
        return remote(cs.at[w, j], cr.at[w, j], c_s.at[w, j], c_r.at[w, j], dev(z, 1 - x, c, y))

    def chain_send():
        nxt = pos + 1
        return remote(cout, cin, ch_s, ch_r, dev(nxt // 2, nxt % 2, c, y))

    def o_send(j):
        return remote(ost.at[j], out_ref.at[:, ds(j * blk + c * bw, bw, bw)], o_s.at[j], o_r.at[j], partner)

    def o_got(j):
        ref = out_ref.at[:, ds(j * blk + (1 - c) * bw, bw, bw)]
        return remote(ost.at[j], ref, o_s.at[j], o_r.at[j], partner)

    def each(n, f):
        def body(i, carry):
            f(i)
            return carry
        lax.fori_loop(0, n, body, 0)

    each(chunks, lambda j: w_local(0, j).start())
    each(chunks, lambda j: te_local(j).start())
    each(halves, lambda jj: t_local(jj).start())
    each(chunks, lambda j: w_local(1, j).start())

    barrier = pltpu.get_barrier_semaphore()

    def greet(where):
        pl.semaphore_signal(barrier, inc=1, device_id=where, device_id_type=MESH)

    greet(partner)
    for dx, dy in peers:
        xx, yy = at_peer(dx, dy)
        greet(dev(z, xx, c, yy))
    line_peers = [
        (z > 0, dev(z - 1, x, c, y)),
        (z < lines - 1, dev(z + 1, x, c, y)),
        ((x == 1) & (z < lines - 1), dev(z + 1, 0, c, y)),
        ((x == 0) & (z > 0), dev(z - 1, 1, c, y)),
    ]
    for there, where in line_peers:
        @pl.when(there)
        def _():
            greet(where)
    pl.semaphore_wait(barrier, 1 + len(peers) + sum(there.astype(jnp.int32) for there, _ in line_peers))

    each(chunks, lambda j: w_swap(0, j).start())
    for dx, dy in peers:
        each(halves, lambda jj: t_send(dx, dy, jj).start())
    each(chunks, lambda j: te_swap(j).start())
    each(halves, lambda jj: t_own(jj).start())
    each(chunks, lambda j: w_swap(1, j).start())

    def own_ready(w, j):
        w_local(w, j).wait()
        w_swap(w, j).wait_recv()

    def own_send(w, j):
        @pl.when(z > 0)
        def _():
            z_send(w, j, z, 0).start()

        @pl.when(z < lines - 1)
        def _():
            z_send(w, j, z, 1).start()

    def forward(w, j, d):
        @pl.when(is_mid & (z + d < lines))
        def _():
            z_send(w, j, z + d, 0).wait_recv()
            z_send(w, j, z + d, 0).start()

        @pl.when(is_mid & (z - d >= 0))
        def _():
            z_send(w, j, z - d, 1).wait_recv()
            z_send(w, j, z - d, 1).start()

    def at_end(w, j):
        for d in range(1, lines):
            @pl.when(z == 0)
            def _():
                z_send(w, j, d, 0).wait_recv()

            @pl.when(z == lines - 1)
            def _():
                z_send(w, j, lines - 1 - d, 0).wait_recv()

    def first_sends(j):
        own_ready(0, j)
        own_send(0, j)

    each(chunks, first_sends)

    def te_ready(j):
        te_local(j).wait()
        te_swap(j).wait_recv()

    each(chunks, te_ready)

    def lay(i, carry):
        for e in range(sub):
            v = te[pl.ds(i * 16, 16), e * LANES:(e + 1) * LANES].astype(F32)
            x2d[pl.ds(i * 16 * sub + e, 16, stride=sub), :] = v
        return carry

    lax.fori_loop(0, two // 16, lay, 0)

    def second_own(j):
        own_ready(1, j)

        @pl.when(jnp.logical_not(is_mid))
        def _():
            own_send(1, j)

    each(chunks, second_own)

    half = dims // 2

    def tile(ref, h):
        return ref[h * sub:(h + 1) * sub, :]

    def step(state, v, q_re, q_im):
        return [(a * re - b * im + v, a * im + b * re) for (re, im), a, b in zip(state, q_re, q_im)]

    def end_half(k):
        hs = range(k * half, (k + 1) * half)
        q_re = [tile(q_re_ref, h) for h in hs]
        q_im = [tile(q_im_ref, h) for h in hs]
        zero = jnp.zeros((sub, LANES), F32)

        def body(i, state):
            for u in range(UNROLL):
                state = step(state, x2d[ds((i * UNROLL + u) * sub, sub, sub), :], q_re, q_im)
            return state

        state = lax.fori_loop(0, two // UNROLL, body, [(zero, zero)] * half)
        for h, (re, im) in zip(hs, state):
            st[0, h * sub:(h + 1) * sub, :] = re
            st[1, h * sub:(h + 1) * sub, :] = im

    end_half(0)
    each(chunks, lambda j: forward(0, j, 1))
    end_half(1)

    def tokens_on(dx, dy):
        def go(jj):
            t_got(dx, dy, jj).wait_recv()
            t_pass(dx, dy, jj).start()
        each(halves, go)

    @pl.when(pos == 0)
    def _():
        cin[...] = jnp.zeros_like(cin)

    @pl.when(pos > 0)
    def _():
        chain_send().wait_recv()

    i_re, i_im = cin[0].astype(F32), cin[1].astype(F32)
    a, b = s_re_ref[...], s_im_ref[...]
    cout[0] = (a * i_re - b * i_im + st[0]).astype(BF16)
    cout[1] = (a * i_im + b * i_re + st[1]).astype(BF16)
    st[0] = i_re
    st[1] = i_im

    @pl.when(pos < 2 * lines - 1)
    def _():
        chain_send().start()

    for dx, dy in peers:
        tokens_on(dx, dy)

    def smooth_half(k):
        hs = range(k * half, (k + 1) * half)
        q_re = [tile(q_re_ref, h) for h in hs]
        q_im = [tile(q_im_ref, h) for h in hs]
        c_re = [tile(c_re_ref, h) for h in hs]
        c_im = [tile(c_im_ref, h) for h in hs]
        skip = skip_ref[...]
        state = [(tile(st.at[0], h), tile(st.at[1], h)) for h in hs]

        def body(i, state):
            for u in range(UNROLL):
                at = ds((i * UNROLL + u) * sub, sub, sub)
                v = x2d[at, :]
                state = step(state, v, q_re, q_im)
                sums = [c_re[h] * state[h][0] - c_im[h] * state[h][1] for h in range(half)]
                while len(sums) > 1:
                    sums = [sum(sums[m:m + 2]) for m in range(0, len(sums), 2)]
                before = v * skip if k == 0 else y2d[at, :]
                y2d[at, :] = before + sums[0]
            return state

        lax.fori_loop(0, two // UNROLL, body, state)

    smooth_half(0)
    for d in range(2, lines - 1):
        each(halves, lambda j: forward(0, j, d))
    smooth_half(1)
    for d in range(2, lines - 1):
        each(halves, lambda j: forward(0, halves + j, d))

    def mid_own(j):
        @pl.when(is_mid)
        def _():
            own_send(1, j)

    def stage(j):
        for d in range(1, lines - 1):
            forward(1, j, d)

    each(halves, mid_own)

    def local_tokens(jj):
        t_local(jj).wait()
        for dx, dy in others:
            t_passed(dx, dy, jj).wait_recv()

    each(halves, local_tokens)

    def project(w, j):
        @pl.when(jnp.logical_not(is_mid))
        def _():
            at_end(w, j)
        right = W[w, j]
        away = jnp.dot(A[w, ds((1 - x) * two, two, two), :], right, preferred_element_type=F32)
        cs[w, j] = away.astype(BF16)
        c_send(w, j).start()
        own[j] = jnp.dot(A[w, ds(x * two, two, two), :], right, preferred_element_type=F32)

    each(chunks, lambda j: project(0, j))
    stage(0)

    def hidden(j):
        c_send(0, j).wait_recv()
        jj = j // 2
        target = j % 2

        def band(i, carry):
            at = pl.ds(pl.multiple_of(i * 16, 16), 16)
            for e in range(tiles):
                lane = slice(e * LANES, (e + 1) * LANES)
                smooth = y2d[pl.ds(i * 16 * sub + j * tiles + e, 16, stride=sub), :]
                gate = own[j, at, lane] + cr[0, j, at, lane].astype(F32)
                value = smooth * jax.nn.sigmoid(smooth) * jax.nn.sigmoid(gate)
                hid[j, at, lane] = value.astype(BF16)
            return carry

        lax.fori_loop(0, two // 16, band, 0)

        @pl.when(target == x)
        def _():
            h_own(jj, j).start()
            for dx, dy in peers:
                if dx == 0:
                    h_send(dx, dy, jj, j).start()
            h_ref(x, y, jj, c)[...] = hid[j]

        @pl.when(target != x)
        def _():
            for dx, dy in peers:
                if dx == 1:
                    h_send(dx, dy, jj, j).start()

    each(halves, hidden)
    stage(1)
    each(halves, lambda j: mid_own(halves + j))
    each(halves, lambda j: hidden(halves + j))

    for dx, dy in peers:
        def hidden_on(jj):
            h_got(dx, dy, jj).wait_recv()
            h_pass(dx, dy, jj).start()
        each(halves, hidden_on)
    each(chunks - 2, lambda j: stage(2 + j))

    def all_hidden(jj):
        for dx, dy in others:
            h_passed(dx, dy, jj).wait_recv()

    each(halves, all_hidden)

    def finish(j):
        c_send(1, j).wait_recv()
        mine = ds(c * rows, rows, rows)
        theirs = ds((1 - c) * rows, rows, rows)
        ost[j] = (own[j, theirs, :] + cr[1, j, theirs, :].astype(F32)).astype(BF16)
        o_send(j).start()
        out_ref[:, ds(j * blk + c * bw, bw, bw)] = (own[j, mine, :] + cr[1, j, mine, :].astype(F32)).astype(BF16)

    project(1, 0)

    def last(j):
        project(1, j + 1)
        finish(j)

    each(chunks - 1, last)
    finish(chunks - 1)
    each(chunks, lambda j: o_got(j).wait_recv())

    def settle(j):
        for w in range(2):
            w_swap(w, j).wait_send()
            c_send(w, j).wait_send()

            @pl.when(z > 0)
            def _():
                z_send(w, j, z, 0).wait_send()

            @pl.when(z < lines - 1)
            def _():
                z_send(w, j, z, 1).wait_send()
            for d in range(1, lines - 1):
                @pl.when(is_mid & (z + d < lines))
                def _():
                    z_send(w, j, z + d, 0).wait_send()

                @pl.when(is_mid & (z - d >= 0))
                def _():
                    z_send(w, j, z - d, 1).wait_send()
        te_swap(j).wait_send()
        o_send(j).wait_send()

    each(chunks, settle)

    def settle_exchange(jj):
        t_own(jj).wait_send()
        h_own(jj, 0).wait_send()
        for dx, dy in peers:
            t_send(dx, dy, jj).wait_send()
            h_send(dx, dy, jj, 0).wait_send()
            t_pass(dx, dy, jj).wait_send()
            h_pass(dx, dy, jj).wait_send()

    each(halves, settle_exchange)

    @pl.when(pos < 2 * lines - 1)
    def _():
        chain_send().wait_send()


def per_device(shards, parts, tokens, decay_rate, angle, in_coef, out_coef, skip_coef, gate_weight, out_weight):
    rows, width = tokens.shape
    dims = decay_rate.shape[1]
    lines = shards // 4
    bw = gate_weight.shape[0]
    blk = 2 * bw
    chunks = width // blk
    assert shards % 4 == 0 and lines > 1 and dims % 2 == 0
    assert chunks % 2 == 0 and bw % LANES == 0 and chunks * 2 * parts == shards
    sub = chunks * bw // LANES
    two = 2 * rows
    depth = lines * blk
    core = lax.axis_index("seq") % 2

    def spread(table):
        table = table.reshape(chunks, 2, bw, dims)
        table = lax.dynamic_index_in_dim(table, core, 1, keepdims=False)
        return table.reshape(chunks * bw, dims).T.reshape(dims * sub, LANES)

    rate = spread(decay_rate)
    theta = spread(angle)
    magnitude = 1.0 - rate
    scaled = spread(in_coef) * jnp.sqrt(1.0 - magnitude * magnitude)
    c_re = scaled * spread(out_coef[0])
    c_im = scaled * spread(out_coef[1])
    q_re = magnitude * jnp.cos(theta)
    q_im = magnitude * jnp.sin(theta)
    span_mag = jnp.exp(two * jnp.log1p(-rate))
    span_re = span_mag * jnp.cos(two * theta)
    span_im = span_mag * jnp.sin(two * theta)
    skip = lax.dynamic_index_in_dim(skip_coef.reshape(chunks, 2, bw), core, 1, keepdims=False).reshape(sub, LANES)

    hbm = pl.BlockSpec(memory_space=pltpu.HBM)
    vmem = pl.BlockSpec(memory_space=pltpu.VMEM)
    dma = pltpu.SemaphoreType.DMA
    halves = chunks // 2
    n = 2 * parts
    flops = 2 * 2 * 4 * rows * depth * chunks * bw
    return pl.pallas_call(
        functools.partial(mixer_kernel, lines, parts, dims),
        in_specs=[hbm] * 3 + [vmem] * 7,
        out_specs=vmem,
        out_shape=jax.ShapeDtypeStruct((rows, width), BF16),
        scratch_shapes=[
            pltpu.VMEM((two, chunks * bw), BF16),
            pltpu.VMEM((two * sub, LANES), F32),
            pltpu.VMEM((two * sub, LANES), F32),
            pltpu.VMEM((2, dims * sub, LANES), F32),
            pltpu.VMEM((2, dims * sub, LANES), BF16),
            pltpu.VMEM((2, dims * sub, LANES), BF16),
            pltpu.VMEM((2, 4 * rows, depth), BF16),
            pltpu.VMEM((2, chunks, depth, bw), BF16),
            pltpu.VMEM((chunks, two, bw), F32),
            pltpu.VMEM((2, chunks, two, bw), BF16),
            pltpu.VMEM((2, chunks, two, bw), BF16),
            pltpu.VMEM((chunks, two, bw), BF16),
            pltpu.VMEM((chunks, rows, bw), BF16),
            dma((2, chunks)),
            dma((chunks,)),
            dma((halves,)),
            dma((2, chunks)),
            dma((2, chunks)),
            dma((chunks,)),
            dma((chunks,)),
            dma((2, 2, chunks, lines)),
            dma((2, chunks, lines)),
            dma((2, n, halves)),
            dma((2, n, halves)),
            dma((2, n, halves)),
            dma((2, n, halves)),
            dma((halves,)),
            dma,
            dma,
            dma((2, chunks)),
            dma((2, chunks)),
            dma((chunks,)),
            dma((chunks,)),
        ],
        compiler_params=pltpu.CompilerParams(
            collective_id=0, has_side_effects=True, vmem_limit_bytes=56 * 1024 * 1024
        ),
        cost_estimate=pl.CostEstimate(flops=flops, bytes_accessed=4 * tokens.size, transcendentals=0),
        name="mixer",
    )(
        tokens, gate_weight, out_weight, q_re, q_im, c_re, c_im, span_re, span_im, skip,
    )


def solution(mesh):
    in_specs = (
        P("seq", "tp"),
        P("tp", None),
        P("tp", None),
        P("tp", None),
        P(None, "tp", None),
        P("tp"),
        P("seq", "tp"),
        P("seq", "tp"),
    )
    body = functools.partial(per_device, mesh.shape["seq"], mesh.shape["tp"])
    return jax.shard_map(body, mesh=mesh, in_specs=in_specs, out_specs=P("seq", "tp"), check_vma=False)
```

time: 296 us -> 182 us (0.61)
  blocking collectives: 160 us -> 0 us
  Pallas kernels: 25.4 us -> 167 us
  waiting for transfers between devices: 66.3 us -> 0 us
  matrix products: 20.6 us -> 0 us
  between operations: 13.5 us -> 0.16 us
  local copies, waits for them, and re-layouts: 5.88 us -> 11.9 us
  other arithmetic: 4.47 us -> 0.54 us
    all_gather x12 -> x0, blocking collectives: 160 us -> none  [small_gather(): done = [lax.all_gather(part, name, axis=axis, tiled=True) for part in parts]]
    pallas_call x2 -> x1, Pallas kernels: 25.4 us -> 167 us  [per_device(): pl.pallas_call(functools.partial(mixer_kernel, lines, parts, dims), in_sp...]
    all_gather x2 -> x0, waiting for transfers between devices: 65 us -> none  [the longest x1 65 us: per_device(): out_all = lax.all_gather(out_weight, 'seq', axis=0, tiled=True)]
    dot_general x2 -> x0, matrix products: 20.6 us -> none  [the longest x1 11.4 us: per_device(): gate_pre = jnp.dot(columns, gate_all, preferred_element_type=jnp.float32)]
    mul x0 -> x12, local copies, waits for them, and re-layouts: none -> 4.09 us  [the longest x2 0.69 us: per_device(): q_re = magnitude * jnp.cos(theta)]
  transfers between devices with their start and end apart: 2 -> 0, of which waited for: 1 -> 0; matrix products, arithmetic and copies ran while one was open for 7% -> 0% of each run, Pallas kernels for 9% -> 0%
where the time goes in v1:
time: 182 us; the launch traced here: 180 us
  Pallas kernels  167 us (92%)
  local copies, waits for them, and re-layouts  11.9 us (7%)
    pallas_call x1, Pallas kernels, per_device(): pl.pallas_call(functools.partial(mixer_kernel, lines, parts, dims), in_sp...  167 us
    unnamed x15, local copies, waits for them, and re-layouts  5.39 us

profile of v1, /device:TPU:0, one launch (start us, length us, event | category | flops | bytes accessed | tf_op | source)
XLA Modules:
  0.0 179.7 jit_solution(1696326949084795246)
XLA Ops:
  0.0 0.0 copy-start.3
  0.0 0.7 copy-done.3
  0.7 0.6 constant_dynamic-slice_fusion
  1.3 1.0 reshape.75
  2.3 0.0 copy-start.1
  2.3 0.1 constant_dynamic-slice_fusion.5
  2.4 0.8 copy-done.1
  3.2 0.1 reshape.76
  3.4 0.8 copy-done.2
  4.1 0.1 reshape.77
  4.3 0.1 constant_dynamic-slice_fusion.3
  4.4 0.7 copy-done
  5.1 0.1 reshape_squeeze.7
  5.2 0.1 reshape_squeeze.6
  5.4 0.1 constant_dynamic-slice_fusion.1
  5.5 0.5 sine_multiply_fusion
  6.1 0.6 reshape.92.s_im_ref
  6.8 0.6 mul.62.q_im_ref
  7.5 0.6 reshape.91.s_re_ref
  8.2 0.6 mul.58.q_re_ref
  9.0 0.6 reshape.93.c_re_ref
  9.7 0.6 reshape.94.c_im_ref
  10.3 167.1 %mixer.1 = bf16[256,2048]{1,0:T(8,128)(2,1)} custom-call(bf16[256,2048]{1,0:T(8,128)(2,1)} %tok.1, bf16[256,2048]{1,0:T(8,128)(2,1)} %gate_w.1, bf16[256,2048]{1,0:T(8,128)(2,1)} %out_w.1, f32[128,128]{1,0:T(8,128)} %mul.58.q_re_ref, f32[128,128]{1,0:T(8,128)} %mul.62.q_im_ref, f32[128,128]{1,0:T(8,128)} %reshape.93.c_re_ref, f32[128,128]{1,0:T(8,128)} %reshape.94.c_im_ref, ...), custom_call_target="tpu_custom_call" | custom-call | flops 8589934592 | bytes 2097152 | tf_op jit(solution)/shard_map/mixer/pallas_call | solution.py:531
  177.4 2.3 %copy.59 = bf16[256,2048]{1,0:T(8,128)(2,1)} copy(bf16[256,2048]{1,0:T(8,128)(2,1)} %mixer.1) | data formatting | bytes 2097152
  (16 shorter events, 0.4 us)
Async XLA Ops:
  0.0 0.7 copy-start.3
  2.3 0.9 copy-start.1
  3.2 0.9 copy-start.2
  4.1 0.9 copy-start

commit v2 on v1

--- a/solution.py
+++ b/solution.py
@@ -15,10 +15,10 @@
 
 def mixer_kernel(
     lines, parts, dims,
-    tok, gate_w, out_w, q_re_ref, q_im_ref, c_re_ref, c_im_ref, s_re_ref, s_im_ref, skip_ref,
+    tok, gate_w, out_w, decay, angle, in_coef, out_coef, skip_in,
     out_ref,
-    te, x2d, y2d, st, cin, cout, A, W, own, cs, cr, hid, ost,
-    l_w, l_te, l_a, sw_s, sw_r, te_s, te_r, z_s, z_r, x_s, x_r, p_s, p_r, po_s, ch_s, ch_r, c_s, c_r, o_s, o_r,
+    raw, q_re_ref, q_im_ref, c_re_ref, c_im_ref, s_re_ref, s_im_ref, skip_ref, te, x2d, y2d, st, cin, cout, A, W, own, cs, cr, hid, ost,
+    l_w, l_te, l_a, l_raw, sw_s, sw_r, te_s, te_r, z_s, z_r, x_s, x_r, p_s, p_r, po_s, ch_s, ch_r, c_s, c_r, o_s, o_r,
 ):
     rows, width = tok.shape
     bw = gate_w.shape[0]
@@ -67,6 +67,11 @@
         return pltpu.make_async_copy(
             tok.at[:, ds(j * blk + c * bw, bw, bw)], te.at[ds(c * rows, rows, rows), ds(j * bw, bw, bw)], l_te.at[j])
 
+    def raw_local(t, j):
+        source = (decay, angle, in_coef, out_coef.at[0], out_coef.at[1])[t]
+        return pltpu.make_async_copy(
+            source.at[:, ds(j * blk + c * bw, bw, bw)], raw.at[t, :, ds(j * bw, bw, bw)], l_raw.at[t, j])
+
     def te_swap(j):
         return remote(
             tok.at[:, ds(j * blk + (1 - c) * bw, bw, bw)],
@@ -171,6 +176,8 @@
 
     each(chunks, lambda j: w_local(0, j).start())
     each(chunks, lambda j: te_local(j).start())
+    for t in range(5):
+        each(chunks, lambda j: raw_local(t, j).start())
     each(halves, lambda jj: t_local(jj).start())
     each(chunks, lambda j: w_local(1, j).start())
 
@@ -241,6 +248,37 @@
         own_send(0, j)
 
     each(chunks, first_sends)
+
+    for t in range(5):
+        each(chunks, lambda j: raw_local(t, j).wait())
+    for e in range(sub):
+        band = slice(e * LANES, (e + 1) * LANES)
+        rate, theta, scale, o_re, o_im = (raw[t, :, band] for t in range(5))
+        magnitude = 1.0 - rate
+        scale = scale * jnp.sqrt(1.0 - magnitude * magnitude)
+        at = pl.ds(e, dims, stride=sub)
+        c_re_ref[at, :] = scale * o_re
+        c_im_ref[at, :] = scale * o_im
+        q_re_ref[at, :] = magnitude * jnp.cos(theta)
+        q_im_ref[at, :] = magnitude * jnp.sin(theta)
+        k, lane = e // tiles, e % tiles
+        row = 2 * k * tiles + lane
+        skip_ref[e:e + 1, :] = jnp.where(c == 0, skip_in[row:row + 1, :], skip_in[row + tiles:row + tiles + 1, :])
+
+    def span_of():
+        base = q_re_ref[...], q_im_ref[...]
+        total = None
+        count = two
+        while count:
+            if count % 2:
+                total = base if total is None else (
+                    total[0] * base[0] - total[1] * base[1], total[0] * base[1] + total[1] * base[0])
+            base = base[0] * base[0] - base[1] * base[1], 2.0 * base[0] * base[1]
+            count //= 2
+        s_re_ref[...] = total[0]
+        s_im_ref[...] = total[1]
+
+    span_of()
 
     def te_ready(j):
         te_local(j).wait()
@@ -502,25 +540,7 @@
     sub = chunks * bw // LANES
     two = 2 * rows
     depth = lines * blk
-    core = lax.axis_index("seq") % 2
-
-    def spread(table):
-        table = table.reshape(chunks, 2, bw, dims)
-        table = lax.dynamic_index_in_dim(table, core, 1, keepdims=False)
-        return table.reshape(chunks * bw, dims).T.reshape(dims * sub, LANES)
-
-    rate = spread(decay_rate)
-    theta = spread(angle)
-    magnitude = 1.0 - rate
-    scaled = spread(in_coef) * jnp.sqrt(1.0 - magnitude * magnitude)
-    c_re = scaled * spread(out_coef[0])
-    c_im = scaled * spread(out_coef[1])
-    q_re = magnitude * jnp.cos(theta)
-    q_im = magnitude * jnp.sin(theta)
-    span_mag = jnp.exp(two * jnp.log1p(-rate))
-    span_re = span_mag * jnp.cos(two * theta)
-    span_im = span_mag * jnp.sin(two * theta)
-    skip = lax.dynamic_index_in_dim(skip_coef.reshape(chunks, 2, bw), core, 1, keepdims=False).reshape(sub, LANES)
+    skip = skip_coef.reshape(2 * sub, LANES)
 
     hbm = pl.BlockSpec(memory_space=pltpu.HBM)
     vmem = pl.BlockSpec(memory_space=pltpu.VMEM)
@@ -530,10 +550,13 @@
     flops = 2 * 2 * 4 * rows * depth * chunks * bw
     return pl.pallas_call(
         functools.partial(mixer_kernel, lines, parts, dims),
-        in_specs=[hbm] * 3 + [vmem] * 7,
+        in_specs=[hbm] * 7 + [vmem],
         out_specs=vmem,
         out_shape=jax.ShapeDtypeStruct((rows, width), BF16),
         scratch_shapes=[
+            pltpu.VMEM((5, dims, chunks * bw), F32),
+        ] + [pltpu.VMEM((dims * sub, LANES), F32)] * 6 + [
+            pltpu.VMEM((sub, LANES), F32),
             pltpu.VMEM((two, chunks * bw), BF16),
             pltpu.VMEM((two * sub, LANES), F32),
             pltpu.VMEM((two * sub, LANES), F32),
@@ -550,6 +573,7 @@
             dma((2, chunks)),
             dma((chunks,)),
             dma((halves,)),
+            dma((5, chunks)),
             dma((2, chunks)),
             dma((2, chunks)),
             dma((chunks,)),
@@ -574,7 +598,7 @@
         cost_estimate=pl.CostEstimate(flops=flops, bytes_accessed=4 * tokens.size, transcendentals=0),
         name="mixer",
     )(
-        tokens, gate_weight, out_weight, q_re, q_im, c_re, c_im, span_re, span_im, skip,
+        tokens, gate_weight, out_weight, decay_rate.T, angle.T, in_coef.T, out_coef.swapaxes(1, 2), skip,
     )
 
 

time: 182 us -> 171 us (0.940)
  local copies, waits for them, and re-layouts: 11.9 us -> 2.3 us
    mul x12 -> x0, local copies, waits for them, and re-layouts: 4.09 us -> none  [the longest x2 0.69 us: per_device(): q_re = magnitude * jnp.cos(theta)]
    unnamed x15 -> x1, local copies, waits for them, and re-layouts: 5.39 us -> 2.3 us
where the time goes in v2:
time: 171 us; the launch traced here: 170 us
  Pallas kernels  167 us (98%)
  local copies, waits for them, and re-layouts  2.3 us (1%)
    pallas_call x1, Pallas kernels, per_device(): pl.pallas_call(functools.partial(mixer_kernel, lines, parts, dims), in_sp...  167 us

profile of v2, /device:TPU:0, one launch (start us, length us, event | category | flops | bytes accessed | tf_op | source)
XLA Modules:
  0.0 169.6 jit_solution(15173785273907896032)
XLA Ops:
  0.0 167.3 %mixer.1 = bf16[256,2048]{1,0:T(8,128)(2,1)} custom-call(bf16[256,2048]{1,0:T(8,128)(2,1)} %tok.1, bf16[256,2048]{1,0:T(8,128)(2,1)} %gate_w.1, bf16[256,2048]{1,0:T(8,128)(2,1)} %out_w.1, f32[16,2048]{1,0:T(8,128)} %bitcast.6, f32[16,2048]{1,0:T(8,128)} %bitcast.7, f32[16,2048]{1,0:T(8,128)} %bitcast.8, f32[2,16,2048]{2,1,0:T(8,128)} %bitcast.5, ...), custom_call_target="tpu_custom_call" | custom-call | flops 8589934592 | bytes 2097152 | tf_op jit(solution)/shard_map/mixer/pallas_call | solution.py:551
  167.3 2.3 %copy.10 = bf16[256,2048]{1,0:T(8,128)(2,1)} copy(bf16[256,2048]{1,0:T(8,128)(2,1)} %mixer.1) | data formatting | bytes 2097152

commit v3 on v2

--- a/solution.py
+++ b/solution.py
@@ -9,16 +9,17 @@
 
 LANES = 128
 UNROLL = 8
+GUESTS = 2
 MESH = pl.DeviceIdType.MESH
 F32, BF16 = jnp.float32, jnp.bfloat16
 
 
 def mixer_kernel(
-    lines, parts, dims,
+    lines, parts, dims, guests,
     tok, gate_w, out_w, decay, angle, in_coef, out_coef, skip_in,
     out_ref,
-    raw, q_re_ref, q_im_ref, c_re_ref, c_im_ref, s_re_ref, s_im_ref, skip_ref, te, x2d, y2d, st, cin, cout, A, W, own, cs, cr, hid, ost,
-    l_w, l_te, l_a, l_raw, sw_s, sw_r, te_s, te_r, z_s, z_r, x_s, x_r, p_s, p_r, po_s, ch_s, ch_r, c_s, c_r, o_s, o_r,
+    raw, q_re_ref, q_im_ref, c_re_ref, c_im_ref, s_re_ref, s_im_ref, skip_ref, te, x2d, y2d, st, cin, cout, A, W, own, own_g, cs, cr, hid, ost, G, bs,
+    l_w, l_te, l_a, l_raw, sw_s, sw_r, te_s, te_r, z_s, z_r, x_s, x_r, p_s, p_r, g_s, g_r, b_s, ch_s, ch_r, c_s, c_r, o_s, o_r,
 ):
     rows, width = tok.shape
     bw = gate_w.shape[0]
@@ -39,6 +40,10 @@
 
     partner = dev(z, x, 1 - c, y)
     is_mid = (z > 0) & (z < lines - 1)
+    is_end = jnp.logical_not(is_mid)
+    is_host = (z == 1) | (z == lines - 2)
+    end_z = jnp.where(z == 1, 0, lines - 1)
+    host_z = jnp.where(z == 0, 1, lines - 2)
 
     def hint(v, m):
         return v if isinstance(v, int) else pl.multiple_of(v, m)
@@ -93,38 +98,51 @@
     def slot(dx, yy):
         return dx * parts + yy
 
-    def t_send(dx, dy, jj):
+    def t_from(g, block):
+        return (G if g else tok).at[:, ds(block * blk, blk, blk)]
+
+    def t_ref(g, xx, cc, yy, jj):
+        return A.at[g, ds((xx * 2 + cc) * rows, rows, rows), a_cols(yy, jj)]
+
+    def t_send(g, dx, dy, jj):
         xx, yy = at_peer(dx, dy)
         return remote(
-            tok.at[:, ds((2 * jj + xx) * blk, blk, blk)],
-            A.at[0, ds((x * 2 + c) * rows, rows, rows), a_cols(y, jj)],
-            x_s.at[0, dx * parts + dy, jj], x_r.at[0, slot(dx, y), jj], dev(z, xx, c, yy))
-
-    def t_got(dx, dy, jj):
-        xx, yy = at_peer(dx, dy)
-        dst = A.at[0, ds((xx * 2 + c) * rows, rows, rows), a_cols(yy, jj)]
-        return remote(dst, dst, x_s.at[0, dx * parts + dy, jj], x_r.at[0, slot(dx, yy), jj], dev(z, xx, c, yy))
+            t_from(g, 2 * jj + xx), t_ref(g, x, c, y, jj),
+            x_s.at[g, dx * parts + dy, jj], x_r.at[g, slot(dx, y), jj], dev(z, xx, c, yy))
+
+    def t_relay(g, dy, jj):
+        xx, yy = at_peer(1, dy)
+        ref = t_ref(g, xx, c, y, jj)
+        return remote(ref, ref, x_s.at[g, parts + dy, jj], x_r.at[g, slot(1, y), jj], dev(z, x, c, yy))
+
+    def t_got(g, dx, dy, jj):
+        xx, yy = at_peer(dx, dy)
+        ref = t_ref(g, xx, c, yy, jj)
+        return remote(ref, ref, x_s.at[g, dx * parts + dy, jj], x_r.at[g, slot(dx, yy), jj], partner)
 
     def t_local(jj):
-        return pltpu.make_async_copy(
-            tok.at[:, ds((2 * jj + x) * blk, blk, blk)],
-            A.at[0, ds((x * 2 + c) * rows, rows, rows), a_cols(y, jj)], l_a.at[jj])
-
-    def t_own(jj):
+        return pltpu.make_async_copy(t_from(0, 2 * jj + x), t_ref(0, x, c, y, jj), l_a.at[jj])
+
+    def t_own(g, jj):
         return remote(
-            tok.at[:, ds((2 * jj + x) * blk, blk, blk)],
-            A.at[0, ds((x * 2 + c) * rows, rows, rows), a_cols(y, jj)],
-            p_s.at[0, 0, jj], p_r.at[0, slot(0, y), jj], partner)
-
-    def t_pass(dx, dy, jj):
-        xx, yy = at_peer(dx, dy)
-        ref = A.at[0, ds((xx * 2 + c) * rows, rows, rows), a_cols(yy, jj)]
-        return remote(ref, ref, p_s.at[0, dx * parts + dy, jj], p_r.at[0, slot(dx, yy), jj], partner)
-
-    def t_passed(dx, dy, jj):
-        xx, yy = at_peer(dx, dy)
-        ref = A.at[0, ds((xx * 2 + 1 - c) * rows, rows, rows), a_cols(yy, jj)]
-        return remote(ref, ref, p_s.at[0, dx * parts + dy, jj], p_r.at[0, slot(dx, yy), jj], partner)
+            t_from(g, 2 * jj + x), t_ref(g, x, c, y, jj), p_s.at[g, 0, jj], p_r.at[g, slot(0, y), jj], partner)
+
+    def t_pass(g, dx, dy, jj):
+        xx, yy = at_peer(dx, dy)
+        ref = t_ref(g, xx, c, yy, jj)
+        return remote(ref, ref, p_s.at[g, dx * parts + dy, jj], p_r.at[g, slot(dx, yy), jj], partner)
+
+    def t_passed(g, dx, dy, jj):
+        xx, yy = at_peer(dx, dy)
+        ref = t_ref(g, xx, 1 - c, yy, jj)
+        return remote(ref, ref, p_s.at[g, dx * parts + dy, jj], p_r.at[g, slot(dx, yy), jj], partner)
+
+    def g_send(k):
+        ref = G.at[:, ds(k * blk, blk, blk)]
+        return remote(t_from(0, k), ref, g_s.at[k], g_r.at[k], dev(host_z, x, c, y))
+
+    def back_send(j):
+        return remote(bs.at[j], cr.at[0, j], b_s.at[j], c_r.at[0, j], dev(end_z, x, c, y))
 
     def h_ref(xx, yy, jj, cc):
         cols = ds((yy * halves + jj) * blk + cc * bw, bw, bw)
@@ -140,6 +158,11 @@
         xx, yy = at_peer(dx, dy)
         ref = h_ref(xx, yy, jj, c)
         return remote(ref, ref, x_s.at[1, dx * parts + dy, jj], x_r.at[1, slot(dx, yy), jj], dev(z, xx, c, yy))
+
+    def h_relay(dy, jj):
+        xx, yy = at_peer(1, dy)
+        ref = h_ref(xx, y, jj, c)
+        return remote(ref, ref, x_s.at[1, parts + dy, jj], x_r.at[1, slot(1, y), jj], dev(z, x, c, yy))
 
     def h_own(jj, j):
         return remote(hid.at[j], h_ref(x, y, jj, c), p_s.at[1, 0, jj], p_r.at[1, slot(0, y), jj], partner)
@@ -203,35 +226,79 @@
     pl.semaphore_wait(barrier, 1 + len(peers) + sum(there.astype(jnp.int32) for there, _ in line_peers))
 
     each(chunks, lambda j: w_swap(0, j).start())
-    for dx, dy in peers:
-        each(halves, lambda jj: t_send(dx, dy, jj).start())
+
+    @pl.when(is_end)
+    def _():
+        each(chunks, lambda k: g_send(k).start())
+
+    def t_start(g):
+        def go(jj):
+            t_send(g, 1, 0, jj).start()
+            for dy in range(1, parts):
+                t_send(g, 0, dy, jj).start()
+            t_own(g, jj).start()
+        each(halves, go)
+
+    t_start(0)
     each(chunks, lambda j: te_swap(j).start())
-    each(halves, lambda jj: t_own(jj).start())
     each(chunks, lambda j: w_swap(1, j).start())
 
     def own_ready(w, j):
         w_local(w, j).wait()
         w_swap(w, j).wait_recv()
 
-    def own_send(w, j):
-        @pl.when(z > 0)
-        def _():
-            z_send(w, j, z, 0).start()
-
-        @pl.when(z < lines - 1)
-        def _():
-            z_send(w, j, z, 1).start()
+    def wanted(w, j, side):
+        target = z + (1 if side else -1)
+        inside = (target >= 0) & (target < lines)
+        if w == 0:
+            inside = inside & (((target > 0) & (target < lines - 1)) | (j >= guests))
+        return inside
+
+    def outer_side(side):
+        target = z + (1 if side else -1)
+        return is_end | (target == 0) | (target == lines - 1)
+
+    def own_outer(w, j):
+        for side in range(2):
+            @pl.when(wanted(w, j, side) & outer_side(side))
+            def _():
+                z_send(w, j, z, side).start()
+
+    def own_inner(w, j):
+        for side in range(2):
+            @pl.when(wanted(w, j, side) & jnp.logical_not(outer_side(side)))
+            def _():
+                z_send(w, j, z, side).start()
+
+    def hop(w, j, o, side, there):
+        @pl.when(there)
+        def _():
+            z_send(w, j, o, side).wait_recv()
+
+            @pl.when(wanted(w, j, side))
+            def _():
+                z_send(w, j, o, side).start()
+
+    def relay_cases(d, from_end):
+        low, high = z - d, z + d
+        if d == 1:
+            at_low = (low == 0) if from_end else (low > 0)
+            at_high = (high == lines - 1) if from_end else (high < lines - 1)
+        else:
+            at_low, at_high = low >= 0, high < lines
+        return (low, 1, is_mid & at_low), (high, 0, is_mid & at_high)
+
+    def forward_end(w, j):
+        for o, side, there in relay_cases(1, True):
+            hop(w, j, o, side, there)
 
     def forward(w, j, d):
-        @pl.when(is_mid & (z + d < lines))
-        def _():
-            z_send(w, j, z + d, 0).wait_recv()
-            z_send(w, j, z + d, 0).start()
-
-        @pl.when(is_mid & (z - d >= 0))
-        def _():
-            z_send(w, j, z - d, 1).wait_recv()
-            z_send(w, j, z - d, 1).start()
+        for o, side, there in relay_cases(d, False):
+            hop(w, j, o, side, there)
+
+    def forward_far(w, j):
+        for d in range(2, lines - 1):
+            forward(w, j, d)
 
     def at_end(w, j):
         for d in range(1, lines):
@@ -245,7 +312,8 @@
 
     def first_sends(j):
         own_ready(0, j)
-        own_send(0, j)
+        own_outer(0, j)
+        own_inner(0, j)
 
     each(chunks, first_sends)
 
@@ -296,12 +364,10 @@
 
     def second_own(j):
         own_ready(1, j)
-
-        @pl.when(jnp.logical_not(is_mid))
-        def _():
-            own_send(1, j)
+        own_outer(1, j)
 
     each(chunks, second_own)
+    each(halves, lambda j: own_inner(1, j))
 
     half = dims // 2
 
@@ -327,15 +393,24 @@
             st[0, h * sub:(h + 1) * sub, :] = re
             st[1, h * sub:(h + 1) * sub, :] = im
 
+    def took_x(g):
+        def go(jj):
+            t_got(g, 1, 0, jj).wait_recv()
+            for dy in range(1, parts):
+                t_relay(g, dy, jj).start()
+            t_pass(g, 1, 0, jj).start()
+        each(halves, go)
+
+    def took_y(g, dx):
+        def go(jj):
+            for dy in range(1, parts):
+                t_got(g, dx, dy, jj).wait_recv()
+                t_pass(g, dx, dy, jj).start()
+        each(halves, go)
+
     end_half(0)
-    each(chunks, lambda j: forward(0, j, 1))
+    took_x(0)
     end_half(1)
-
-    def tokens_on(dx, dy):
-        def go(jj):
-            t_got(dx, dy, jj).wait_recv()
-            t_pass(dx, dy, jj).start()
-        each(halves, go)
 
     @pl.when(pos == 0)
     def _():
@@ -356,8 +431,16 @@
     def _():
         chain_send().start()
 
-    for dx, dy in peers:
-        tokens_on(dx, dy)
+    took_y(0, 0)
+
+    @pl.when(is_host)
+    def _():
+        each(chunks, lambda k: g_send(k).wait_recv())
+        t_start(2)
+
+        def keep(jj):
+            t_ref(2, x, c, y, jj)[...] = t_from(2, 2 * jj + x)[...]
+        each(halves, keep)
 
     def smooth_half(k):
         hs = range(k * half, (k + 1) * half)
@@ -383,42 +466,81 @@
         lax.fori_loop(0, two // UNROLL, body, state)
 
     smooth_half(0)
-    for d in range(2, lines - 1):
-        each(halves, lambda j: forward(0, j, d))
+    took_y(0, 1)
+    each(chunks, lambda j: forward(0, j, 1))
     smooth_half(1)
-    for d in range(2, lines - 1):
-        each(halves, lambda j: forward(0, halves + j, d))
-
-    def mid_own(j):
-        @pl.when(is_mid)
-        def _():
-            own_send(1, j)
-
-    def stage(j):
-        for d in range(1, lines - 1):
-            forward(1, j, d)
-
-    each(halves, mid_own)
-
-    def local_tokens(jj):
-        t_local(jj).wait()
-        for dx, dy in others:
-            t_passed(dx, dy, jj).wait_recv()
-
-    each(halves, local_tokens)
-
-    def project(w, j):
-        @pl.when(jnp.logical_not(is_mid))
-        def _():
-            at_end(w, j)
+    each(halves, lambda j: forward(1, j, 1))
+
+    @pl.when(is_host)
+    def _():
+        took_x(2)
+        took_y(2, 0)
+
+    def all_tokens(g):
+        def go(jj):
+            for dx, dy in others:
+                t_passed(g, dx, dy, jj).wait_recv()
+        each(halves, go)
+
+    each(halves, lambda jj: t_local(jj).wait())
+    all_tokens(0)
+
+    def multiply(w, g, k, j, mine):
         right = W[w, j]
-        away = jnp.dot(A[w, ds((1 - x) * two, two, two), :], right, preferred_element_type=F32)
-        cs[w, j] = away.astype(BF16)
-        c_send(w, j).start()
-        own[j] = jnp.dot(A[w, ds(x * two, two, two), :], right, preferred_element_type=F32)
-
-    each(chunks, lambda j: project(0, j))
-    stage(0)
+        away = jnp.dot(A[g, ds((1 - x) * two, two, two), :], right, preferred_element_type=F32)
+        cs[k, j] = away.astype(BF16)
+        c_send(k, j).start()
+        mine[j] = jnp.dot(A[g, ds(x * two, two, two), :], right, preferred_element_type=F32)
+
+    def project(j):
+        forward_far(0, j)
+
+        @pl.when(is_end & (j >= guests))
+        def _():
+            at_end(0, j)
+
+        @pl.when(is_mid | (j >= guests))
+        def _():
+            multiply(0, 0, 0, j, own)
+
+        @pl.when(is_end & (j < guests))
+        def _():
+            own[j] = jnp.zeros((two, bw), F32)
+
+    each(halves, lambda j: forward_end(0, j))
+
+    def first_project(j):
+        @pl.when(halves + j < chunks)
+        def _():
+            forward_end(0, halves + j)
+        project(j)
+
+    each(guests, first_project)
+
+    @pl.when(is_host)
+    def _():
+        took_y(2, 1)
+        all_tokens(2)
+        each(guests, lambda j: multiply(0, 2, 2, j, own_g))
+
+    def guest_back(j):
+        @pl.when(is_host)
+        def _():
+            c_send(2, j).wait_recv()
+            bs[j] = (own_g[j] + cr[2, j].astype(F32)).astype(BF16)
+            back_send(j).start()
+
+    def later_project(j):
+        @pl.when((halves + j >= halves + guests) & (halves + j < chunks))
+        def _():
+            forward_end(0, halves + j)
+        project(j)
+
+    each(1, guest_back)
+    lax.fori_loop(guests, chunks, lambda j, n: (later_project(j), n)[1], 0)
+    lax.fori_loop(1, guests, lambda j, n: (guest_back(j), n)[1], 0)
+    each(halves, lambda j: forward_end(1, j))
+    own_inner(1, halves)
 
     def hidden(j):
         c_send(0, j).wait_recv()
@@ -440,28 +562,37 @@
         @pl.when(target == x)
         def _():
             h_own(jj, j).start()
-            for dx, dy in peers:
-                if dx == 0:
-                    h_send(dx, dy, jj, j).start()
+            for dy in range(1, parts):
+                h_send(0, dy, jj, j).start()
             h_ref(x, y, jj, c)[...] = hid[j]
 
         @pl.when(target != x)
         def _():
-            for dx, dy in peers:
-                if dx == 1:
-                    h_send(dx, dy, jj, j).start()
+            h_send(1, 0, jj, j).start()
 
     each(halves, hidden)
-    stage(1)
-    each(halves, lambda j: mid_own(halves + j))
+    forward_end(1, halves)
+    lax.fori_loop(halves + 1, chunks, lambda j, n: (own_inner(1, j), n)[1], 0)
     each(halves, lambda j: hidden(halves + j))
-
-    for dx, dy in peers:
-        def hidden_on(jj):
-            h_got(dx, dy, jj).wait_recv()
-            h_pass(dx, dy, jj).start()
-        each(halves, hidden_on)
-    each(chunks - 2, lambda j: stage(2 + j))
+    lax.fori_loop(halves + 1, chunks, lambda j, n: (forward_end(1, j), n)[1], 0)
+
+    def hidden_x(jj):
+        h_got(1, 0, jj).wait_recv()
+        for dy in range(1, parts):
+            h_relay(dy, jj).start()
+        h_pass(1, 0, jj).start()
+
+    def hidden_y(dx):
+        def go(jj):
+            for dy in range(1, parts):
+                h_got(dx, dy, jj).wait_recv()
+                h_pass(dx, dy, jj).start()
+        each(halves, go)
+
+    each(halves, hidden_x)
+    each(halves, lambda j: forward_far(1, j))
+    hidden_y(0)
+    hidden_y(1)
 
     def all_hidden(jj):
         for dx, dy in others:
@@ -477,10 +608,21 @@
         o_send(j).start()
         out_ref[:, ds(j * blk + c * bw, bw, bw)] = (own[j, mine, :] + cr[1, j, mine, :].astype(F32)).astype(BF16)
 
-    project(1, 0)
+    def mix(j):
+        @pl.when(j >= halves)
+        def _():
+            forward(1, j, 1)
+            forward_far(1, j)
+
+        @pl.when(is_end)
+        def _():
+            at_end(1, j)
+        multiply(1, 1, 1, j, own)
+
+    mix(0)
 
     def last(j):
-        project(1, j + 1)
+        mix(j + 1)
         finish(j)
 
     each(chunks - 1, last)
@@ -490,38 +632,61 @@
     def settle(j):
         for w in range(2):
             w_swap(w, j).wait_send()
-            c_send(w, j).wait_send()
-
-            @pl.when(z > 0)
-            def _():
-                z_send(w, j, z, 0).wait_send()
-
-            @pl.when(z < lines - 1)
-            def _():
-                z_send(w, j, z, 1).wait_send()
+            for side in range(2):
+                @pl.when(wanted(w, j, side))
+                def _():
+                    z_send(w, j, z, side).wait_send()
             for d in range(1, lines - 1):
-                @pl.when(is_mid & (z + d < lines))
-                def _():
-                    z_send(w, j, z + d, 0).wait_send()
-
-                @pl.when(is_mid & (z - d >= 0))
-                def _():
-                    z_send(w, j, z - d, 1).wait_send()
+                for o, side, there in ((z - d, 1, z - d >= 0), (z + d, 0, z + d < lines)):
+                    @pl.when(is_mid & there & wanted(w, j, side))
+                    def _():
+                        z_send(w, j, o, side).wait_send()
         te_swap(j).wait_send()
         o_send(j).wait_send()
+        c_send(1, j).wait_send()
+
+        @pl.when(is_mid | (j >= guests))
+        def _():
+            c_send(0, j).wait_send()
+
+        @pl.when(is_host & (j < guests))
+        def _():
+            c_send(2, j).wait_send()
+            back_send(j).wait_send()
+
+        @pl.when(is_end)
+        def _():
+            g_send(j).wait_send()
 
     each(chunks, settle)
 
-    def settle_exchange(jj):
-        t_own(jj).wait_send()
+    def settle_tokens(g):
+        def go(jj):
+            t_own(g, jj).wait_send()
+            t_send(g, 1, 0, jj).wait_send()
+            for dy in range(1, parts):
+                t_send(g, 0, dy, jj).wait_send()
+                t_relay(g, dy, jj).wait_send()
+            for dx, dy in peers:
+                t_pass(g, dx, dy, jj).wait_send()
+        each(halves, go)
+
+    settle_tokens(0)
+
+    @pl.when(is_host)
+    def _():
+        settle_tokens(2)
+
+    def settle_hidden(jj):
         h_own(jj, 0).wait_send()
+        h_send(1, 0, jj, 0).wait_send()
+        for dy in range(1, parts):
+            h_send(0, dy, jj, 0).wait_send()
+            h_relay(dy, jj).wait_send()
         for dx, dy in peers:
-            t_send(dx, dy, jj).wait_send()
-            h_send(dx, dy, jj, 0).wait_send()
-            t_pass(dx, dy, jj).wait_send()
             h_pass(dx, dy, jj).wait_send()
 
-    each(halves, settle_exchange)
+    each(halves, settle_hidden)
 
     @pl.when(pos < 2 * lines - 1)
     def _():
@@ -535,7 +700,7 @@
     bw = gate_weight.shape[0]
     blk = 2 * bw
     chunks = width // blk
-    assert shards % 4 == 0 and lines > 1 and dims % 2 == 0
+    assert shards % 4 == 0 and lines > 3 and dims % 2 == 0
     assert chunks % 2 == 0 and bw % LANES == 0 and chunks * 2 * parts == shards
     sub = chunks * bw // LANES
     two = 2 * rows
@@ -549,7 +714,7 @@
     n = 2 * parts
     flops = 2 * 2 * 4 * rows * depth * chunks * bw
     return pl.pallas_call(
-        functools.partial(mixer_kernel, lines, parts, dims),
+        functools.partial(mixer_kernel, lines, parts, dims, max(1, chunks * GUESTS // 4)),
         in_specs=[hbm] * 7 + [vmem],
         out_specs=vmem,
         out_shape=jax.ShapeDtypeStruct((rows, width), BF16),
@@ -563,13 +728,16 @@
             pltpu.VMEM((2, dims * sub, LANES), F32),
             pltpu.VMEM((2, dims * sub, LANES), BF16),
             pltpu.VMEM((2, dims * sub, LANES), BF16),
-            pltpu.VMEM((2, 4 * rows, depth), BF16),
+            pltpu.VMEM((3, 4 * rows, depth), BF16),
             pltpu.VMEM((2, chunks, depth, bw), BF16),
             pltpu.VMEM((chunks, two, bw), F32),
-            pltpu.VMEM((2, chunks, two, bw), BF16),
-            pltpu.VMEM((2, chunks, two, bw), BF16),
+            pltpu.VMEM((chunks, two, bw), F32),
+            pltpu.VMEM((3, chunks, two, bw), BF16),
+            pltpu.VMEM((3, chunks, two, bw), BF16),
             pltpu.VMEM((chunks, two, bw), BF16),
             pltpu.VMEM((chunks, rows, bw), BF16),
+            pltpu.VMEM((rows, width), BF16),
+            pltpu.VMEM((chunks, two, bw), BF16),
             dma((2, chunks)),
             dma((chunks,)),
             dma((halves,)),
@@ -580,15 +748,17 @@
             dma((chunks,)),
             dma((2, 2, chunks, lines)),
             dma((2, chunks, lines)),
-            dma((2, n, halves)),
-            dma((2, n, halves)),
-            dma((2, n, halves)),
-            dma((2, n, halves)),
-            dma((halves,)),
+            dma((3, n, halves)),
+            dma((3, n, halves)),
+            dma((3, n, halves)),
+            dma((3, n, halves)),
+            dma((chunks,)),
+            dma((chunks,)),
+            dma((chunks,)),
             dma,
             dma,
-            dma((2, chunks)),
-            dma((2, chunks)),
+            dma((3, chunks)),
+            dma((3, chunks)),
             dma((chunks,)),
             dma((chunks,)),
         ],

time: 171 us -> 212 us (1.24)
  Pallas kernels: 167 us -> 209 us
    pallas_call x1, Pallas kernels: 167 us -> 209 us  [per_device(): pl.pallas_call(functools.partial(mixer_kernel, lines, parts, dims, max(1,...]
where the time goes in v3:
time: 212 us; the launch traced here: 211 us
  Pallas kernels  209 us (99%)
  local copies, waits for them, and re-layouts  2.3 us (1%)
    pallas_call x1, Pallas kernels, per_device(): pl.pallas_call(functools.partial(mixer_kernel, lines, parts, dims, max(1,...  209 us

profile of v3, /device:TPU:0, one launch (start us, length us, event | category | flops | bytes accessed | tf_op | source)
XLA Modules:
  0.0 211.3 jit_solution(6294396514796409463)
XLA Ops:
  0.0 208.9 %mixer.1 = bf16[256,2048]{1,0:T(8,128)(2,1)} custom-call(bf16[256,2048]{1,0:T(8,128)(2,1)} %tok.1, bf16[256,2048]{1,0:T(8,128)(2,1)} %gate_w.1, bf16[256,2048]{1,0:T(8,128)(2,1)} %out_w.1, f32[16,2048]{1,0:T(8,128)} %bitcast.6, f32[16,2048]{1,0:T(8,128)} %bitcast.7, f32[16,2048]{1,0:T(8,128)} %bitcast.8, f32[2,16,2048]{2,1,0:T(8,128)} %bitcast.5, ...), custom_call_target="tpu_custom_call" | custom-call | flops 8589934592 | bytes 2097152 | tf_op jit(solution)/shard_map/mixer/pallas_call | solution.py:716
  209.0 2.3 %copy.10 = bf16[256,2048]{1,0:T(8,128)(2,1)} copy(bf16[256,2048]{1,0:T(8,128)(2,1)} %mixer.1) | data formatting | bytes 2097152

commit v4 on v3

--- a/solution.py
+++ b/solution.py
@@ -15,7 +15,7 @@
 
 
 def mixer_kernel(
-    lines, parts, dims, guests,
+    lines, parts, dims, kept,
     tok, gate_w, out_w, decay, angle, in_coef, out_coef, skip_in,
     out_ref,
     raw, q_re_ref, q_im_ref, c_re_ref, c_im_ref, s_re_ref, s_im_ref, skip_ref, te, x2d, y2d, st, cin, cout, A, W, own, own_g, cs, cr, hid, ost, G, bs,
@@ -227,19 +227,13 @@
 
     each(chunks, lambda j: w_swap(0, j).start())
 
-    @pl.when(is_end)
-    def _():
-        each(chunks, lambda k: g_send(k).start())
-
-    def t_start(g):
-        def go(jj):
-            t_send(g, 1, 0, jj).start()
-            for dy in range(1, parts):
-                t_send(g, 0, dy, jj).start()
-            t_own(g, jj).start()
-        each(halves, go)
-
-    t_start(0)
+    def t_start(g, jj):
+        t_send(g, 1, 0, jj).start()
+        for dy in range(1, parts):
+            t_send(g, 0, dy, jj).start()
+        t_own(g, jj).start()
+
+    each(halves, lambda jj: t_start(0, jj))
     each(chunks, lambda j: te_swap(j).start())
     each(chunks, lambda j: w_swap(1, j).start())
 
@@ -251,18 +245,17 @@
         target = z + (1 if side else -1)
         inside = (target >= 0) & (target < lines)
         if w == 0:
-            inside = inside & (((target > 0) & (target < lines - 1)) | (j >= guests))
+            inside = inside & (((target > 0) & (target < lines - 1)) | (j < kept))
         return inside
 
     def outer_side(side):
         target = z + (1 if side else -1)
         return is_end | (target == 0) | (target == lines - 1)
 
-    def own_outer(w, j):
-        for side in range(2):
-            @pl.when(wanted(w, j, side) & outer_side(side))
-            def _():
-                z_send(w, j, z, side).start()
+    def own_at(w, j, side, there):
+        @pl.when(wanted(w, j, side) & there)
+        def _():
+            z_send(w, j, z, side).start()
 
     def own_inner(w, j):
         for side in range(2):
@@ -288,9 +281,10 @@
             at_low, at_high = low >= 0, high < lines
         return (low, 1, is_mid & at_low), (high, 0, is_mid & at_high)
 
-    def forward_end(w, j):
+    def forward_end(w, j, sides=(0, 1)):
         for o, side, there in relay_cases(1, True):
-            hop(w, j, o, side, there)
+            if side in sides:
+                hop(w, j, o, side, there)
 
     def forward(w, j, d):
         for o, side, there in relay_cases(d, False):
@@ -310,12 +304,29 @@
             def _():
                 z_send(w, j, lines - 1 - d, 0).wait_recv()
 
+    def span(start, stop, f):
+        def body(j, carry):
+            f(j)
+            return carry
+        lax.fori_loop(start, stop, body, 0)
+
     def first_sends(j):
         own_ready(0, j)
-        own_outer(0, j)
-        own_inner(0, j)
-
-    each(chunks, first_sends)
+        own_at(0, j, 0, z >= 0)
+        own_at(0, j, 1, z >= 0)
+
+    each(halves, first_sends)
+
+    @pl.when(z == lines - 1)
+    def _():
+        each(chunks, lambda k: g_send(k).start())
+
+    def next_sends(j):
+        own_ready(0, j)
+        own_at(0, j, 0, outer_side(0))
+        own_at(0, j, 1, is_mid & outer_side(1))
+
+    span(halves, chunks, next_sends)
 
     for t in range(5):
         each(chunks, lambda j: raw_local(t, j).wait())
@@ -364,10 +375,11 @@
 
     def second_own(j):
         own_ready(1, j)
-        own_outer(1, j)
+        for side in range(2):
+            own_at(1, j, side, is_mid & outer_side(side) & (j == 0))
+        own_at(1, j, 0, z == lines - 1)
 
     each(chunks, second_own)
-    each(halves, lambda j: own_inner(1, j))
 
     half = dims // 2
 
@@ -409,8 +421,12 @@
         each(halves, go)
 
     end_half(0)
+    end_half(1)
     took_x(0)
-    end_half(1)
+    inner_left = jnp.logical_not(outer_side(0))
+    each(halves, lambda j: forward_end(0, j, (0,)))
+    span(halves, chunks, lambda j: own_at(0, j, 0, inner_left))
+    own_at(1, 0, 0, is_mid & inner_left)
 
     @pl.when(pos == 0)
     def _():
@@ -431,16 +447,24 @@
     def _():
         chain_send().start()
 
+    @pl.when(z == 0)
+    def _():
+        each(chunks, lambda k: g_send(k).start())
+
+    inner_right = is_mid & jnp.logical_not(outer_side(1))
+    each(halves, lambda j: forward_end(0, j, (1,)))
+    span(halves, chunks, lambda j: own_at(0, j, 1, (z == 0) | inner_right))
+    each(chunks, lambda j: own_at(1, j, 1, (z == 0) | (inner_right & (j == 0))))
+    each(halves, lambda j: forward(0, j, 1))
     took_y(0, 0)
 
-    @pl.when(is_host)
-    def _():
-        each(chunks, lambda k: g_send(k).wait_recv())
-        t_start(2)
-
-        def keep(jj):
+    def guest_tokens(jj):
+        @pl.when(is_host)
+        def _():
+            g_send(2 * jj).wait_recv()
+            g_send(2 * jj + 1).wait_recv()
+            t_start(2, jj)
             t_ref(2, x, c, y, jj)[...] = t_from(2, 2 * jj + x)[...]
-        each(halves, keep)
 
     def smooth_half(k):
         hs = range(k * half, (k + 1) * half)
@@ -467,14 +491,17 @@
 
     smooth_half(0)
     took_y(0, 1)
-    each(chunks, lambda j: forward(0, j, 1))
+    each(halves, lambda j: forward_far(0, j))
+
+    def rest_outer(j):
+        for side in range(2):
+            own_at(1, j, side, is_mid & outer_side(side))
+
+    span(1, chunks, rest_outer)
+    guest_tokens(0)
     smooth_half(1)
-    each(halves, lambda j: forward(1, j, 1))
-
-    @pl.when(is_host)
-    def _():
-        took_x(2)
-        took_y(2, 0)
+    span(1, halves, guest_tokens)
+    span(halves, chunks, lambda j: forward(0, j, 1))
 
     def all_tokens(g):
         def go(jj):
@@ -493,35 +520,57 @@
         mine[j] = jnp.dot(A[g, ds(x * two, two, two), :], right, preferred_element_type=F32)
 
     def project(j):
+        @pl.when(is_end & (j < kept))
+        def _():
+            at_end(0, j)
+
+        @pl.when(is_mid | (j < kept))
+        def _():
+            multiply(0, 0, 0, j, own)
+
+        @pl.when(is_end & (j >= kept))
+        def _():
+            own[j] = jnp.zeros((two, bw), F32)
+
+    each(halves, project)
+
+    @pl.when(is_host)
+    def _():
+        took_x(2)
+
+    span(halves, chunks, lambda j: forward_end(0, j))
+    span(1, chunks, lambda j: own_inner(1, j))
+
+    @pl.when(is_host)
+    def _():
+        took_y(2, 0)
+
+    forward(1, 0, 1)
+
+    def later_project(j):
         forward_far(0, j)
-
-        @pl.when(is_end & (j >= guests))
-        def _():
-            at_end(0, j)
-
-        @pl.when(is_mid | (j >= guests))
-        def _():
-            multiply(0, 0, 0, j, own)
-
-        @pl.when(is_end & (j < guests))
-        def _():
-            own[j] = jnp.zeros((two, bw), F32)
-
-    each(halves, lambda j: forward_end(0, j))
-
-    def first_project(j):
-        @pl.when(halves + j < chunks)
-        def _():
-            forward_end(0, halves + j)
         project(j)
 
-    each(guests, first_project)
+    span(halves, kept, later_project)
+    forward_far(0, kept)
 
     @pl.when(is_host)
     def _():
         took_y(2, 1)
         all_tokens(2)
-        each(guests, lambda j: multiply(0, 2, 2, j, own_g))
+        multiply(0, 2, 2, kept, own_g)
+
+    def guest_sums(j):
+        forward_far(0, j)
+
+        @pl.when(is_host)
+        def _():
+            multiply(0, 2, 2, j, own_g)
+
+    span(kept + 1, chunks, guest_sums)
+    span(1, halves, lambda j: forward(1, j, 1))
+    each(halves, lambda j: forward_end(1, j))
+    span(kept, chunks, project)
 
     def guest_back(j):
         @pl.when(is_host)
@@ -529,18 +578,6 @@
             c_send(2, j).wait_recv()
             bs[j] = (own_g[j] + cr[2, j].astype(F32)).astype(BF16)
             back_send(j).start()
-
-    def later_project(j):
-        @pl.when((halves + j >= halves + guests) & (halves + j < chunks))
-        def _():
-            forward_end(0, halves + j)
-        project(j)
-
-    each(1, guest_back)
-    lax.fori_loop(guests, chunks, lambda j, n: (later_project(j), n)[1], 0)
-    lax.fori_loop(1, guests, lambda j, n: (guest_back(j), n)[1], 0)
-    each(halves, lambda j: forward_end(1, j))
-    own_inner(1, halves)
 
     def hidden(j):
         c_send(0, j).wait_recv()
@@ -570,29 +607,32 @@
         def _():
             h_send(1, 0, jj, j).start()
 
-    each(halves, hidden)
-    forward_end(1, halves)
-    lax.fori_loop(halves + 1, chunks, lambda j, n: (own_inner(1, j), n)[1], 0)
-    each(halves, lambda j: hidden(halves + j))
-    lax.fori_loop(halves + 1, chunks, lambda j, n: (forward_end(1, j), n)[1], 0)
-
     def hidden_x(jj):
         h_got(1, 0, jj).wait_recv()
         for dy in range(1, parts):
             h_relay(dy, jj).start()
         h_pass(1, 0, jj).start()
 
-    def hidden_y(dx):
-        def go(jj):
-            for dy in range(1, parts):
-                h_got(dx, dy, jj).wait_recv()
-                h_pass(dx, dy, jj).start()
-        each(halves, go)
-
-    each(halves, hidden_x)
-    each(halves, lambda j: forward_far(1, j))
-    hidden_y(0)
-    hidden_y(1)
+    def hidden_y(dx, jj):
+        for dy in range(1, parts):
+            h_got(dx, dy, jj).wait_recv()
+            h_pass(dx, dy, jj).start()
+
+    each(halves, hidden)
+    span(kept, chunks, guest_back)
+    span(halves, chunks, lambda j: forward(1, j, 1))
+    span(halves, chunks, lambda j: forward_end(1, j))
+    span(0, halves // 2, hidden_x)
+    forward_far(1, 0)
+    span(0, halves // 2, lambda jj: hidden_y(0, jj))
+    span(halves, chunks, hidden)
+    span(1, halves, lambda j: forward_far(1, j))
+    span(halves // 2, halves, hidden_x)
+    span(0, halves // 2, lambda jj: hidden_y(1, jj))
+    span(halves // 2, halves, lambda jj: hidden_y(0, jj))
+    forward_far(1, halves)
+    span(halves // 2, halves, lambda jj: hidden_y(1, jj))
+    span(halves + 1, chunks, lambda j: forward_far(1, j))
 
     def all_hidden(jj):
         for dx, dy in others:
@@ -609,11 +649,6 @@
         out_ref[:, ds(j * blk + c * bw, bw, bw)] = (own[j, mine, :] + cr[1, j, mine, :].astype(F32)).astype(BF16)
 
     def mix(j):
-        @pl.when(j >= halves)
-        def _():
-            forward(1, j, 1)
-            forward_far(1, j)
-
         @pl.when(is_end)
         def _():
             at_end(1, j)
@@ -645,11 +680,11 @@
         o_send(j).wait_send()
         c_send(1, j).wait_send()
 
-        @pl.when(is_mid | (j >= guests))
+        @pl.when(is_mid | (j < kept))
         def _():
             c_send(0, j).wait_send()
 
-        @pl.when(is_host & (j < guests))
+        @pl.when(is_host & (j >= kept))
         def _():
             c_send(2, j).wait_send()
             back_send(j).wait_send()
@@ -714,7 +749,7 @@
     n = 2 * parts
     flops = 2 * 2 * 4 * rows * depth * chunks * bw
     return pl.pallas_call(
-        functools.partial(mixer_kernel, lines, parts, dims, max(1, chunks * GUESTS // 4)),
+        functools.partial(mixer_kernel, lines, parts, dims, chunks - max(1, chunks * GUESTS // 4)),
         in_specs=[hbm] * 7 + [vmem],
         out_specs=vmem,
         out_shape=jax.ShapeDtypeStruct((rows, width), BF16),

time: 212 us -> 151 us (0.71)
  the two profiles are of different devices: /device:TPU:0 before, /device:TPU:11 now
where the time goes in v4:
time: 151 us
  Pallas kernels  149 us (99%)
  local copies, waits for them, and re-layouts  2.3 us (2%)
    pallas_call x1, Pallas kernels, per_device(): pl.pallas_call(functools.partial(mixer_kernel, lines, parts, dims, chunks...  149 us

profile of v4, /device:TPU:11, one launch (start us, length us, event | category | flops | bytes accessed | tf_op | source)
XLA Modules:
  0.0 151.3 jit_solution(5632318590491739351)
XLA Ops:
  0.0 149.0 %mixer.1 = bf16[256,2048]{1,0:T(8,128)(2,1)} custom-call(bf16[256,2048]{1,0:T(8,128)(2,1)} %tok.1, bf16[256,2048]{1,0:T(8,128)(2,1)} %gate_w.1, bf16[256,2048]{1,0:T(8,128)(2,1)} %out_w.1, f32[16,2048]{1,0:T(8,128)} %bitcast.6, f32[16,2048]{1,0:T(8,128)} %bitcast.7, f32[16,2048]{1,0:T(8,128)} %bitcast.8, f32[2,16,2048]{2,1,0:T(8,128)} %bitcast.5, ...), custom_call_target="tpu_custom_call" | custom-call | flops 8589934592 | bytes 2097152 | tf_op jit(solution)/shard_map/mixer/pallas_call | solution.py:751
  149.0 2.3 %copy.10 = bf16[256,2048]{1,0:T(8,128)(2,1)} copy(bf16[256,2048]{1,0:T(8,128)(2,1)} %mixer.1) | data formatting | bytes 2097152

commit v5 on v4

--- a/solution.py
+++ b/solution.py
@@ -18,8 +18,8 @@
     lines, parts, dims, kept,
     tok, gate_w, out_w, decay, angle, in_coef, out_coef, skip_in,
     out_ref,
-    raw, q_re_ref, q_im_ref, c_re_ref, c_im_ref, s_re_ref, s_im_ref, skip_ref, te, x2d, y2d, st, cin, cout, A, W, own, own_g, cs, cr, hid, ost, G, bs,
-    l_w, l_te, l_a, l_raw, sw_s, sw_r, te_s, te_r, z_s, z_r, x_s, x_r, p_s, p_r, g_s, g_r, b_s, ch_s, ch_r, c_s, c_r, o_s, o_r,
+    raw, q_re_ref, q_im_ref, c_re_ref, c_im_ref, s_re_ref, s_im_ref, skip_ref, te, x2d, y2d, st, ein, eout, cin, cout, A, W, own, own_g, cs, cr, hid, ost, G, bs,
+    l_w, l_te, l_a, l_raw, sw_s, sw_r, te_s, te_r, z_s, z_r, x_s, x_r, p_s, p_r, g_s, g_r, b_s, e_s, e_r, ch_s, ch_r, c_s, c_r, o_s, o_r,
 ):
     rows, width = tok.shape
     bw = gate_w.shape[0]
@@ -33,7 +33,6 @@
     s = lax.axis_index("seq")
     y = lax.axis_index("tp")
     z, x, c = s // 4, (s // 2) % 2, s % 2
-    pos = z * 2 + x
 
     def dev(zz, xx, cc, yy):
         return ((zz * 2 + xx) * 2 + cc, yy)
@@ -180,9 +179,11 @@
     def c_send(w, j):
         return remote(cs.at[w, j], cr.at[w, j], c_s.at[w, j], c_r.at[w, j], dev(z, 1 - x, c, y))
 
+    def e_send():
+        return remote(eout, ein, e_s, e_r, dev(z, 1 - x, c, y))
+
     def chain_send():
-        nxt = pos + 1
-        return remote(cout, cin, ch_s, ch_r, dev(nxt // 2, nxt % 2, c, y))
+        return remote(cout, cin, ch_s, ch_r, dev(z + 1, x, c, y))
 
     def o_send(j):
         return remote(ost.at[j], out_ref.at[:, ds(j * blk + c * bw, bw, bw)], o_s.at[j], o_r.at[j], partner)
@@ -216,8 +217,6 @@
     line_peers = [
         (z > 0, dev(z - 1, x, c, y)),
         (z < lines - 1, dev(z + 1, x, c, y)),
-        ((x == 1) & (z < lines - 1), dev(z + 1, 0, c, y)),
-        ((x == 0) & (z > 0), dev(z - 1, 1, c, y)),
     ]
     for there, where in line_peers:
         @pl.when(there)
@@ -226,6 +225,14 @@
     pl.semaphore_wait(barrier, 1 + len(peers) + sum(there.astype(jnp.int32) for there, _ in line_peers))
 
     each(chunks, lambda j: w_swap(0, j).start())
+
+    @pl.when(z == 0)
+    def _():
+        each(halves, lambda k: g_send(k).start())
+
+    @pl.when(z == lines - 1)
+    def _():
+        each(chunks, lambda k: g_send(k).start())
 
     def t_start(g, jj):
         t_send(g, 1, 0, jj).start()
@@ -313,20 +320,9 @@
     def first_sends(j):
         own_ready(0, j)
         own_at(0, j, 0, z >= 0)
-        own_at(0, j, 1, z >= 0)
-
-    each(halves, first_sends)
-
-    @pl.when(z == lines - 1)
-    def _():
-        each(chunks, lambda k: g_send(k).start())
-
-    def next_sends(j):
-        own_ready(0, j)
-        own_at(0, j, 0, outer_side(0))
-        own_at(0, j, 1, is_mid & outer_side(1))
-
-    span(halves, chunks, next_sends)
+        own_at(0, j, 1, is_mid & (outer_side(1) | (j < halves)))
+
+    each(chunks, first_sends)
 
     for t in range(5):
         each(chunks, lambda j: raw_local(t, j).wait())
@@ -422,38 +418,51 @@
 
     end_half(0)
     end_half(1)
+    eout[...] = st[...].astype(BF16)
+    e_send().start()
     took_x(0)
     inner_left = jnp.logical_not(outer_side(0))
-    each(halves, lambda j: forward_end(0, j, (0,)))
-    span(halves, chunks, lambda j: own_at(0, j, 0, inner_left))
-    own_at(1, 0, 0, is_mid & inner_left)
-
-    @pl.when(pos == 0)
+    own_at(1, 0, 0, inner_left)
+
+    def cmul(a, b):
+        return a[0] * b[0] - a[1] * b[1], a[0] * b[1] + a[1] * b[0]
+
+    span_q = s_re_ref[...], s_im_ref[...]
+    e_send().wait_recv()
+    mine = st[0], st[1]
+    other = ein[0].astype(F32), ein[1].astype(F32)
+    first = [jnp.where(x == 0, m, o) for m, o in zip(mine, other)]
+    second = [jnp.where(x == 0, o, m) for m, o in zip(mine, other)]
+    plane = [a + b for a, b in zip(cmul(span_q, first), second)]
+
+    @pl.when(z == 0)
     def _():
         cin[...] = jnp.zeros_like(cin)
 
-    @pl.when(pos > 0)
+    @pl.when(z > 0)
     def _():
         chain_send().wait_recv()
 
-    i_re, i_im = cin[0].astype(F32), cin[1].astype(F32)
-    a, b = s_re_ref[...], s_im_ref[...]
-    cout[0] = (a * i_re - b * i_im + st[0]).astype(BF16)
-    cout[1] = (a * i_im + b * i_re + st[1]).astype(BF16)
-    st[0] = i_re
-    st[1] = i_im
-
-    @pl.when(pos < 2 * lines - 1)
+    carry = cin[0].astype(F32), cin[1].astype(F32)
+    moved = cmul(span_q, carry)
+    onward = [a + b for a, b in zip(cmul(span_q, moved), plane)]
+    cout[0] = onward[0].astype(BF16)
+    cout[1] = onward[1].astype(BF16)
+
+    @pl.when(z < lines - 1)
     def _():
         chain_send().start()
 
+    for k in range(2):
+        st[k] = jnp.where(x == 0, carry[k], moved[k] + first[k])
+
+    inner_right = is_mid & jnp.logical_not(outer_side(1))
+
     @pl.when(z == 0)
     def _():
-        each(chunks, lambda k: g_send(k).start())
-
-    inner_right = is_mid & jnp.logical_not(outer_side(1))
-    each(halves, lambda j: forward_end(0, j, (1,)))
-    span(halves, chunks, lambda j: own_at(0, j, 1, (z == 0) | inner_right))
+        each(halves, lambda k: g_send(halves + k).start())
+
+    each(chunks, lambda j: own_at(0, j, 1, (z == 0) | (inner_right & (j >= halves))))
     each(chunks, lambda j: own_at(1, j, 1, (z == 0) | (inner_right & (j == 0))))
     each(halves, lambda j: forward(0, j, 1))
     took_y(0, 0)
@@ -489,28 +498,11 @@
 
         lax.fori_loop(0, two // UNROLL, body, state)
 
-    smooth_half(0)
-    took_y(0, 1)
-    each(halves, lambda j: forward_far(0, j))
-
-    def rest_outer(j):
-        for side in range(2):
-            own_at(1, j, side, is_mid & outer_side(side))
-
-    span(1, chunks, rest_outer)
-    guest_tokens(0)
-    smooth_half(1)
-    span(1, halves, guest_tokens)
-    span(halves, chunks, lambda j: forward(0, j, 1))
-
     def all_tokens(g):
         def go(jj):
             for dx, dy in others:
                 t_passed(g, dx, dy, jj).wait_recv()
         each(halves, go)
-
-    each(halves, lambda jj: t_local(jj).wait())
-    all_tokens(0)
 
     def multiply(w, g, k, j, mine):
         right = W[w, j]
@@ -532,45 +524,30 @@
         def _():
             own[j] = jnp.zeros((two, bw), F32)
 
-    each(halves, project)
+    guest_tokens(0)
+    smooth_half(0)
+    took_y(0, 1)
+
+    def rest_outer(j):
+        for side in range(2):
+            own_at(1, j, side, is_mid & outer_side(side))
+
+    rest_outer(1)
+    each(halves, lambda j: forward_end(0, j, (0,)))
+    span(1, halves, guest_tokens)
+    smooth_half(1)
+
+    forward_end(0, 0, (1,))
 
     @pl.when(is_host)
     def _():
         took_x(2)
-
-    span(halves, chunks, lambda j: forward_end(0, j))
-    span(1, chunks, lambda j: own_inner(1, j))
-
-    @pl.when(is_host)
-    def _():
         took_y(2, 0)
 
     forward(1, 0, 1)
-
-    def later_project(j):
-        forward_far(0, j)
-        project(j)
-
-    span(halves, kept, later_project)
-    forward_far(0, kept)
-
-    @pl.when(is_host)
-    def _():
-        took_y(2, 1)
-        all_tokens(2)
-        multiply(0, 2, 2, kept, own_g)
-
-    def guest_sums(j):
-        forward_far(0, j)
-
-        @pl.when(is_host)
-        def _():
-            multiply(0, 2, 2, j, own_g)
-
-    span(kept + 1, chunks, guest_sums)
-    span(1, halves, lambda j: forward(1, j, 1))
-    each(halves, lambda j: forward_end(1, j))
-    span(kept, chunks, project)
+    span(1, halves, lambda j: forward_end(0, j, (1,)))
+    each(halves, lambda jj: t_local(jj).wait())
+    all_tokens(0)
 
     def guest_back(j):
         @pl.when(is_host)
@@ -618,21 +595,68 @@
             h_got(dx, dy, jj).wait_recv()
             h_pass(dx, dy, jj).start()
 
-    each(halves, hidden)
-    span(kept, chunks, guest_back)
-    span(halves, chunks, lambda j: forward(1, j, 1))
+    def early_project(j):
+        forward_far(0, j)
+        project(j)
+        forward_end(0, halves + j)
+
+    each(halves, early_project)
+    span(2, chunks, rest_outer)
+    own_inner(1, 1)
+    span(halves, chunks, lambda j: forward(0, j, 1))
+
+    @pl.when(is_host)
+    def _():
+        took_y(2, 1)
+        all_tokens(2)
+
+    @pl.when(is_end)
+    def _():
+        each(halves, hidden)
+
+    def guest_sums(j):
+        forward_far(0, j)
+
+        @pl.when(is_host & (j >= kept))
+        def _():
+            multiply(0, 2, 2, j, own_g)
+
+    def guest_step(j):
+        guest_sums(j)
+        forward_end(1, j - halves)
+
+    span(halves, chunks, guest_step)
+    span(2, chunks, lambda j: own_inner(1, j))
+
+    @pl.when(is_mid)
+    def _():
+        each(halves, hidden)
+
+    def late_project(j):
+        project(j)
+
+        @pl.when(j >= kept)
+        def _():
+            guest_back(j)
+
+    span(halves, chunks, late_project)
+    span(1, halves, lambda j: forward(1, j, 1))
+
+    each(halves, lambda j: forward_far(1, j))
     span(halves, chunks, lambda j: forward_end(1, j))
     span(0, halves // 2, hidden_x)
-    forward_far(1, 0)
     span(0, halves // 2, lambda jj: hidden_y(0, jj))
-    span(halves, chunks, hidden)
-    span(1, halves, lambda j: forward_far(1, j))
+    span(0, halves // 2, lambda jj: hidden_y(1, jj))
+
+
+    def gate_done(j):
+        hidden(j)
+        forward(1, j, 1)
+
+    span(halves, chunks, gate_done)
     span(halves // 2, halves, hidden_x)
-    span(0, halves // 2, lambda jj: hidden_y(1, jj))
     span(halves // 2, halves, lambda jj: hidden_y(0, jj))
-    forward_far(1, halves)
     span(halves // 2, halves, lambda jj: hidden_y(1, jj))
-    span(halves + 1, chunks, lambda j: forward_far(1, j))
 
     def all_hidden(jj):
         for dx, dy in others:
@@ -649,6 +673,10 @@
         out_ref[:, ds(j * blk + c * bw, bw, bw)] = (own[j, mine, :] + cr[1, j, mine, :].astype(F32)).astype(BF16)
 
     def mix(j):
+        @pl.when(halves + j < chunks)
+        def _():
+            forward_far(1, halves + j)
+
         @pl.when(is_end)
         def _():
             at_end(1, j)
@@ -723,7 +751,9 @@
 
     each(halves, settle_hidden)
 
-    @pl.when(pos < 2 * lines - 1)
+    e_send().wait_send()
+
+    @pl.when(z < lines - 1)
     def _():
         chain_send().wait_send()
 
@@ -761,6 +791,8 @@
             pltpu.VMEM((two * sub, LANES), F32),
             pltpu.VMEM((two * sub, LANES), F32),
             pltpu.VMEM((2, dims * sub, LANES), F32),
+            pltpu.VMEM((2, dims * sub, LANES), BF16),
+            pltpu.VMEM((2, dims * sub, LANES), BF16),
             pltpu.VMEM((2, dims * sub, LANES), BF16),
             pltpu.VMEM((2, dims * sub, LANES), BF16),
             pltpu.VMEM((3, 4 * rows, depth), BF16),
@@ -792,6 +824,8 @@
             dma((chunks,)),
             dma,
             dma,
+            dma,
+            dma,
             dma((3, chunks)),
             dma((3, chunks)),
             dma((chunks,)),

time: 151 us -> 141 us (0.934)
  the two profiles are of different devices: /device:TPU:11 before, /device:TPU:0 now
where the time goes in v5:
time: 141 us; the launch traced here: 140 us
  Pallas kernels  137 us (97%)
  local copies, waits for them, and re-layouts  2.3 us (2%)
    pallas_call x1, Pallas kernels, per_device(): pl.pallas_call(functools.partial(mixer_kernel, lines, parts, dims, chunks...  137 us

profile of v5, /device:TPU:0, one launch (start us, length us, event | category | flops | bytes accessed | tf_op | source)
XLA Modules:
  0.0 139.5 jit_solution(10185065400969310660)
XLA Ops:
  0.0 137.2 %mixer.1 = bf16[256,2048]{1,0:T(8,128)(2,1)} custom-call(bf16[256,2048]{1,0:T(8,128)(2,1)} %tok.1, bf16[256,2048]{1,0:T(8,128)(2,1)} %gate_w.1, bf16[256,2048]{1,0:T(8,128)(2,1)} %out_w.1, f32[16,2048]{1,0:T(8,128)} %bitcast.6, f32[16,2048]{1,0:T(8,128)} %bitcast.7, f32[16,2048]{1,0:T(8,128)} %bitcast.8, f32[2,16,2048]{2,1,0:T(8,128)} %bitcast.5, ...), custom_call_target="tpu_custom_call" | custom-call | flops 8589934592 | bytes 2097152 | tf_op jit(solution)/shard_map/mixer/pallas_call | solution.py:781
  137.2 2.3 %copy.10 = bf16[256,2048]{1,0:T(8,128)(2,1)} copy(bf16[256,2048]{1,0:T(8,128)(2,1)} %mixer.1) | data formatting | bytes 2097152

commit v6 on v5

--- a/solution.py
+++ b/solution.py
@@ -228,7 +228,7 @@
 
     @pl.when(z == 0)
     def _():
-        each(halves, lambda k: g_send(k).start())
+        each(chunks - 1, lambda k: g_send(k).start())
 
     @pl.when(z == lines - 1)
     def _():
@@ -293,9 +293,10 @@
             if side in sides:
                 hop(w, j, o, side, there)
 
-    def forward(w, j, d):
+    def forward(w, j, d, sides=(0, 1)):
         for o, side, there in relay_cases(d, False):
-            hop(w, j, o, side, there)
+            if side in sides:
+                hop(w, j, o, side, there)
 
     def forward_far(w, j):
         for d in range(2, lines - 1):
@@ -372,7 +373,7 @@
     def second_own(j):
         own_ready(1, j)
         for side in range(2):
-            own_at(1, j, side, is_mid & outer_side(side) & (j == 0))
+            own_at(1, j, side, is_mid & outer_side(side) & (j < halves))
         own_at(1, j, 0, z == lines - 1)
 
     each(chunks, second_own)
@@ -460,10 +461,10 @@
 
     @pl.when(z == 0)
     def _():
-        each(halves, lambda k: g_send(halves + k).start())
+        g_send(chunks - 1).start()
 
     each(chunks, lambda j: own_at(0, j, 1, (z == 0) | (inner_right & (j >= halves))))
-    each(chunks, lambda j: own_at(1, j, 1, (z == 0) | (inner_right & (j == 0))))
+    each(chunks, lambda j: own_at(1, j, 1, z == 0))
     each(halves, lambda j: forward(0, j, 1))
     took_y(0, 0)
 
@@ -475,7 +476,7 @@
             t_start(2, jj)
             t_ref(2, x, c, y, jj)[...] = t_from(2, 2 * jj + x)[...]
 
-    def smooth_half(k):
+    def smooth_half(k, part, parts_of):
         hs = range(k * half, (k + 1) * half)
         q_re = [tile(q_re_ref, h) for h in hs]
         q_im = [tile(q_im_ref, h) for h in hs]
@@ -496,7 +497,12 @@
                 y2d[at, :] = before + sums[0]
             return state
 
-        lax.fori_loop(0, two // UNROLL, body, state)
+        steps = two // UNROLL // parts_of
+        state = lax.fori_loop(part * steps, (part + 1) * steps, body, state)
+        if part + 1 < parts_of:
+            for h, (re, im) in zip(hs, state):
+                st[0, h * sub:(h + 1) * sub, :] = re
+                st[1, h * sub:(h + 1) * sub, :] = im
 
     def all_tokens(g):
         def go(jj):
@@ -525,26 +531,26 @@
             own[j] = jnp.zeros((two, bw), F32)
 
     guest_tokens(0)
-    smooth_half(0)
+    smooth_half(0, 0, 1)
     took_y(0, 1)
 
     def rest_outer(j):
         for side in range(2):
             own_at(1, j, side, is_mid & outer_side(side))
 
-    rest_outer(1)
-    each(halves, lambda j: forward_end(0, j, (0,)))
+    rest_outer(halves)
+    forward_end(0, 0, (0,))
     span(1, halves, guest_tokens)
-    smooth_half(1)
-
+    smooth_half(1, 0, 2)
+    span(1, halves, lambda j: forward_end(0, j, (0,)))
     forward_end(0, 0, (1,))
+    smooth_half(1, 1, 2)
 
     @pl.when(is_host)
     def _():
         took_x(2)
         took_y(2, 0)
 
-    forward(1, 0, 1)
     span(1, halves, lambda j: forward_end(0, j, (1,)))
     each(halves, lambda jj: t_local(jj).wait())
     all_tokens(0)
@@ -597,12 +603,14 @@
 
     def early_project(j):
         forward_far(0, j)
+        forward_end(0, halves + j)
         project(j)
-        forward_end(0, halves + j)
 
     each(halves, early_project)
-    span(2, chunks, rest_outer)
+    span(halves + 1, chunks, rest_outer)
+    own_at(1, 0, 1, inner_right)
     own_inner(1, 1)
+    forward(1, 0, 1, (0,))
     span(halves, chunks, lambda j: forward(0, j, 1))
 
     @pl.when(is_host)
@@ -626,6 +634,7 @@
         forward_end(1, j - halves)
 
     span(halves, chunks, guest_step)
+    forward(1, 0, 1, (1,))
     span(2, chunks, lambda j: own_inner(1, j))
 
     @pl.when(is_mid)
@@ -641,20 +650,17 @@
 
     span(halves, chunks, late_project)
     span(1, halves, lambda j: forward(1, j, 1))
-
-    each(halves, lambda j: forward_far(1, j))
+    forward_far(1, 0)
+    span(0, halves // 2, hidden_x)
+    hidden(halves)
+    span(1, halves, lambda j: forward_far(1, j))
+    span(halves + 1, chunks, hidden)
     span(halves, chunks, lambda j: forward_end(1, j))
-    span(0, halves // 2, hidden_x)
     span(0, halves // 2, lambda jj: hidden_y(0, jj))
     span(0, halves // 2, lambda jj: hidden_y(1, jj))
-
-
-    def gate_done(j):
-        hidden(j)
-        forward(1, j, 1)
-
-    span(halves, chunks, gate_done)
+    forward(1, halves, 1)
     span(halves // 2, halves, hidden_x)
+    span(halves + 1, chunks, lambda j: forward(1, j, 1))
     span(halves // 2, halves, lambda jj: hidden_y(0, jj))
     span(halves // 2, halves, lambda jj: hidden_y(1, jj))
 

time: 141 us -> 137 us (0.972)
  Pallas kernels: 137 us -> 133 us
    pallas_call x1, Pallas kernels: 137 us -> 133 us  [per_device(): pl.pallas_call(functools.partial(mixer_kernel, lines, parts, dims, chunks...]
where the time goes in v6:
time: 137 us; the launch traced here: 136 us
  Pallas kernels  133 us (97%)
  local copies, waits for them, and re-layouts  2.3 us (2%)
    pallas_call x1, Pallas kernels, per_device(): pl.pallas_call(functools.partial(mixer_kernel, lines, parts, dims, chunks...  133 us

profile of v6, /device:TPU:0, one launch (start us, length us, event | category | flops | bytes accessed | tf_op | source)
XLA Modules:
  0.0 135.5 jit_solution(8806844550996697686)
XLA Ops:
  0.0 133.2 %mixer.1 = bf16[256,2048]{1,0:T(8,128)(2,1)} custom-call(bf16[256,2048]{1,0:T(8,128)(2,1)} %tok.1, bf16[256,2048]{1,0:T(8,128)(2,1)} %gate_w.1, bf16[256,2048]{1,0:T(8,128)(2,1)} %out_w.1, f32[16,2048]{1,0:T(8,128)} %bitcast.6, f32[16,2048]{1,0:T(8,128)} %bitcast.7, f32[16,2048]{1,0:T(8,128)} %bitcast.8, f32[2,16,2048]{2,1,0:T(8,128)} %bitcast.5, ...), custom_call_target="tpu_custom_call" | custom-call | flops 8589934592 | bytes 2097152 | tf_op jit(solution)/shard_map/mixer/pallas_call | solution.py:787
  133.2 2.3 %copy.10 = bf16[256,2048]{1,0:T(8,128)(2,1)} copy(bf16[256,2048]{1,0:T(8,128)(2,1)} %mixer.1) | data formatting | bytes 2097152

commit v7 on v6

--- a/solution.py
+++ b/solution.py
@@ -18,8 +18,8 @@
     lines, parts, dims, kept,
     tok, gate_w, out_w, decay, angle, in_coef, out_coef, skip_in,
     out_ref,
-    raw, q_re_ref, q_im_ref, c_re_ref, c_im_ref, s_re_ref, s_im_ref, skip_ref, te, x2d, y2d, st, ein, eout, cin, cout, A, W, own, own_g, cs, cr, hid, ost, G, bs,
-    l_w, l_te, l_a, l_raw, sw_s, sw_r, te_s, te_r, z_s, z_r, x_s, x_r, p_s, p_r, g_s, g_r, b_s, e_s, e_r, ch_s, ch_r, c_s, c_r, o_s, o_r,
+    raw, q_re_ref, q_im_ref, c_re_ref, c_im_ref, s_re_ref, s_im_ref, skip_ref, te, x2d, y2d, st, ein, eout, cin, cout, A, W, own, own_g, cs, cr, hid, ost, omine, G, bs,
+    l_w, l_te, l_a, l_raw, sw_s, sw_r, te_s, te_r, z_s, z_r, x_s, x_r, p_s, p_r, g_s, g_r, b_s, e_s, e_r, ch_s, ch_r, c_s, c_r, o_s, o_r, o_l,
 ):
     rows, width = tok.shape
     bw = gate_w.shape[0]
@@ -147,21 +147,27 @@
         cols = ds((yy * halves + jj) * blk + cc * bw, bw, bw)
         return A.at[1, ds(xx * two, two, two), cols]
 
-    def h_send(dx, dy, jj, j):
+    def h_band(xx, yy, jj, r):
+        cols = ds((yy * halves + jj) * blk + c * bw, bw, bw)
+        return A.at[1, ds(xx * two + r * rows, rows, rows), cols]
+
+    def h_send(dx, dy, jj, j, r):
         xx, yy = at_peer(dx, dy)
         return remote(
-            hid.at[j], h_ref(x, y, jj, c), x_s.at[1, dx * parts + dy, jj], x_r.at[1, slot(dx, y), jj],
-            dev(z, xx, c, yy))
-
-    def h_got(dx, dy, jj):
+            hid.at[j, ds(r * rows, rows, rows)], h_band(x, y, jj, r),
+            x_s.at[1 + 2 * r, dx * parts + dy, jj], x_r.at[1 + 2 * r, slot(dx, y), jj], dev(z, xx, c, yy))
+
+    def h_got(dx, dy, jj, r):
         xx, yy = at_peer(dx, dy)
-        ref = h_ref(xx, yy, jj, c)
-        return remote(ref, ref, x_s.at[1, dx * parts + dy, jj], x_r.at[1, slot(dx, yy), jj], dev(z, xx, c, yy))
-
-    def h_relay(dy, jj):
+        ref = h_band(xx, yy, jj, r)
+        return remote(
+            ref, ref, x_s.at[1 + 2 * r, dx * parts + dy, jj], x_r.at[1 + 2 * r, slot(dx, yy), jj], dev(z, xx, c, yy))
+
+    def h_relay(dy, jj, r):
         xx, yy = at_peer(1, dy)
-        ref = h_ref(xx, y, jj, c)
-        return remote(ref, ref, x_s.at[1, parts + dy, jj], x_r.at[1, slot(1, y), jj], dev(z, x, c, yy))
+        ref = h_band(xx, y, jj, r)
+        return remote(
+            ref, ref, x_s.at[1 + 2 * r, parts + dy, jj], x_r.at[1 + 2 * r, slot(1, y), jj], dev(z, x, c, yy))
 
     def h_own(jj, j):
         return remote(hid.at[j], h_ref(x, y, jj, c), p_s.at[1, 0, jj], p_r.at[1, slot(0, y), jj], partner)
@@ -187,6 +193,9 @@
 
     def o_send(j):
         return remote(ost.at[j], out_ref.at[:, ds(j * blk + c * bw, bw, bw)], o_s.at[j], o_r.at[j], partner)
+
+    def o_keep(j):
+        return pltpu.make_async_copy(omine.at[j], out_ref.at[:, ds(j * blk + c * bw, bw, bw)], o_l.at[j])
 
     def o_got(j):
         ref = out_ref.at[:, ds(j * blk + (1 - c) * bw, bw, bw)]
@@ -538,7 +547,7 @@
         for side in range(2):
             own_at(1, j, side, is_mid & outer_side(side))
 
-    rest_outer(halves)
+    span(halves, chunks, rest_outer)
     forward_end(0, 0, (0,))
     span(1, halves, guest_tokens)
     smooth_half(1, 0, 2)
@@ -577,28 +586,34 @@
                 hid[j, at, lane] = value.astype(BF16)
             return carry
 
-        lax.fori_loop(0, two // 16, band, 0)
+        for r in range(2):
+            lax.fori_loop(r * rows // 16, (r + 1) * rows // 16, band, 0)
+
+            @pl.when(target == x)
+            def _():
+                for dy in range(1, parts):
+                    h_send(0, dy, jj, j, r).start()
+
+            @pl.when(target != x)
+            def _():
+                h_send(1, 0, jj, j, r).start()
 
         @pl.when(target == x)
         def _():
             h_own(jj, j).start()
+            h_ref(x, y, jj, c)[...] = hid[j]
+
+    def hidden_x(jj):
+        for r in range(2):
+            h_got(1, 0, jj, r).wait_recv()
             for dy in range(1, parts):
-                h_send(0, dy, jj, j).start()
-            h_ref(x, y, jj, c)[...] = hid[j]
-
-        @pl.when(target != x)
-        def _():
-            h_send(1, 0, jj, j).start()
-
-    def hidden_x(jj):
-        h_got(1, 0, jj).wait_recv()
-        for dy in range(1, parts):
-            h_relay(dy, jj).start()
+                h_relay(dy, jj, r).start()
         h_pass(1, 0, jj).start()
 
     def hidden_y(dx, jj):
         for dy in range(1, parts):
-            h_got(dx, dy, jj).wait_recv()
+            for r in range(2):
+                h_got(dx, dy, jj, r).wait_recv()
             h_pass(dx, dy, jj).start()
 
     def early_project(j):
@@ -607,7 +622,6 @@
         project(j)
 
     each(halves, early_project)
-    span(halves + 1, chunks, rest_outer)
     own_at(1, 0, 1, inner_right)
     own_inner(1, 1)
     forward(1, 0, 1, (0,))
@@ -676,7 +690,8 @@
         theirs = ds((1 - c) * rows, rows, rows)
         ost[j] = (own[j, theirs, :] + cr[1, j, theirs, :].astype(F32)).astype(BF16)
         o_send(j).start()
-        out_ref[:, ds(j * blk + c * bw, bw, bw)] = (own[j, mine, :] + cr[1, j, mine, :].astype(F32)).astype(BF16)
+        omine[j] = (own[j, mine, :] + cr[1, j, mine, :].astype(F32)).astype(BF16)
+        o_keep(j).start()
 
     def mix(j):
         @pl.when(halves + j < chunks)
@@ -696,6 +711,7 @@
 
     each(chunks - 1, last)
     finish(chunks - 1)
+    each(chunks, lambda j: o_keep(j).wait())
     each(chunks, lambda j: o_got(j).wait_recv())
 
     def settle(j):
@@ -748,10 +764,11 @@
 
     def settle_hidden(jj):
         h_own(jj, 0).wait_send()
-        h_send(1, 0, jj, 0).wait_send()
-        for dy in range(1, parts):
-            h_send(0, dy, jj, 0).wait_send()
-            h_relay(dy, jj).wait_send()
+        for r in range(2):
+            h_send(1, 0, jj, 0, r).wait_send()
+            for dy in range(1, parts):
+                h_send(0, dy, jj, 0, r).wait_send()
+                h_relay(dy, jj, r).wait_send()
         for dx, dy in peers:
             h_pass(dx, dy, jj).wait_send()
 
@@ -787,7 +804,7 @@
     return pl.pallas_call(
         functools.partial(mixer_kernel, lines, parts, dims, chunks - max(1, chunks * GUESTS // 4)),
         in_specs=[hbm] * 7 + [vmem],
-        out_specs=vmem,
+        out_specs=hbm,
         out_shape=jax.ShapeDtypeStruct((rows, width), BF16),
         scratch_shapes=[
             pltpu.VMEM((5, dims, chunks * bw), F32),
@@ -809,6 +826,7 @@
             pltpu.VMEM((3, chunks, two, bw), BF16),
             pltpu.VMEM((chunks, two, bw), BF16),
             pltpu.VMEM((chunks, rows, bw), BF16),
+            pltpu.VMEM((chunks, rows, bw), BF16),
             pltpu.VMEM((rows, width), BF16),
             pltpu.VMEM((chunks, two, bw), BF16),
             dma((2, chunks)),
@@ -821,8 +839,8 @@
             dma((chunks,)),
             dma((2, 2, chunks, lines)),
             dma((2, chunks, lines)),
-            dma((3, n, halves)),
-            dma((3, n, halves)),
+            dma((4, n, halves)),
+            dma((4, n, halves)),
             dma((3, n, halves)),
             dma((3, n, halves)),
             dma((chunks,)),
@@ -836,6 +854,7 @@
             dma((3, chunks)),
             dma((chunks,)),
             dma((chunks,)),
+            dma((chunks,)),
         ],
         compiler_params=pltpu.CompilerParams(
             collective_id=0, has_side_effects=True, vmem_limit_bytes=56 * 1024 * 1024

time: 137 us -> 136 us (level)
  no operation moved by 1% of the time
where the time goes in v7:
time: 136 us; the launch traced here: 135 us
  Pallas kernels  133 us (98%)
  local copies, waits for them, and re-layouts  2.3 us (2%)
    pallas_call x1, Pallas kernels, per_device(): pl.pallas_call(functools.partial(mixer_kernel, lines, parts, dims, chunks...  133 us

profile of v7, /device:TPU:0, one launch (start us, length us, event | category | flops | bytes accessed | tf_op | source)
XLA Modules:
  0.0 134.8 jit_solution(18173710625911291264)
XLA Ops:
  0.0 132.5 %mixer.1 = bf16[256,2048]{1,0:T(8,128)(2,1)} custom-call(bf16[256,2048]{1,0:T(8,128)(2,1)} %tok.1, bf16[256,2048]{1,0:T(8,128)(2,1)} %gate_w.1, bf16[256,2048]{1,0:T(8,128)(2,1)} %out_w.1, f32[16,2048]{1,0:T(8,128)} %bitcast.6, f32[16,2048]{1,0:T(8,128)} %bitcast.7, f32[16,2048]{1,0:T(8,128)} %bitcast.8, f32[2,16,2048]{2,1,0:T(8,128)} %bitcast.5, ...), custom_call_target="tpu_custom_call" | custom-call | flops 8589934592 | bytes 2097152 | tf_op jit(solution)/shard_map/mixer/pallas_call | solution.py:804
  132.5 2.3 %copy.10 = bf16[256,2048]{1,0:T(8,128)(2,1)} copy(bf16[256,2048]{1,0:T(8,128)(2,1)} %mixer.1) | data formatting | bytes 2097152

commit v8 on v7

--- a/solution.py
+++ b/solution.py
@@ -65,28 +65,28 @@
     def w_swap(w, j):
         return remote(
             weights[w].at[:, ds(j * blk + (1 - c) * bw, bw, bw)],
-            W.at[w, j, ds(z * blk + c * bw, bw, bw)], sw_s.at[w, j], sw_r.at[w, j], partner)
+            W.at[w, j, ds(z * blk + c * bw, bw, bw)], sw_s.at[w], sw_r.at[w, j], partner)
 
     def te_local(j):
         return pltpu.make_async_copy(
-            tok.at[:, ds(j * blk + c * bw, bw, bw)], te.at[ds(c * rows, rows, rows), ds(j * bw, bw, bw)], l_te.at[j])
+            tok.at[:, ds(j * blk + c * bw, bw, bw)], te.at[ds(c * rows, rows, rows), ds(j * bw, bw, bw)], l_te)
 
     def raw_local(t, j):
         source = (decay, angle, in_coef, out_coef.at[0], out_coef.at[1])[t]
         return pltpu.make_async_copy(
-            source.at[:, ds(j * blk + c * bw, bw, bw)], raw.at[t, :, ds(j * bw, bw, bw)], l_raw.at[t, j])
+            source.at[:, ds(j * blk + c * bw, bw, bw)], raw.at[t, :, ds(j * bw, bw, bw)], l_raw)
 
     def te_swap(j):
         return remote(
             tok.at[:, ds(j * blk + (1 - c) * bw, bw, bw)],
-            te.at[ds(c * rows, rows, rows), ds(j * bw, bw, bw)], te_s.at[j], te_r.at[j], partner)
+            te.at[ds(c * rows, rows, rows), ds(j * bw, bw, bw)], te_s, te_r, partner)
 
     def piece(w, j, o):
         return W.at[w, j, ds(o * blk, blk, blk)]
 
     def z_send(w, j, o, side):
         where = dev(z + (1 if side else -1), x, c, y)
-        return remote(piece(w, j, o), piece(w, j, o), z_s.at[side, w, j, o], z_r.at[w, j, o], where)
+        return remote(piece(w, j, o), piece(w, j, o), z_s.at[side, w], z_r.at[w, j, o], where)
 
     def at_peer(dx, dy):
         return (x + dx) % 2, (y + dy) % parts
@@ -138,10 +138,10 @@
 
     def g_send(k):
         ref = G.at[:, ds(k * blk, blk, blk)]
-        return remote(t_from(0, k), ref, g_s.at[k], g_r.at[k], dev(host_z, x, c, y))
+        return remote(t_from(0, k), ref, g_s, g_r.at[k], dev(host_z, x, c, y))
 
     def back_send(j):
-        return remote(bs.at[j], cr.at[0, j], b_s.at[j], c_r.at[0, j], dev(end_z, x, c, y))
+        return remote(bs.at[j], cr.at[0, j], b_s, c_r.at[0, j], dev(end_z, x, c, y))
 
     def h_ref(xx, yy, jj, cc):
         cols = ds((yy * halves + jj) * blk + cc * bw, bw, bw)
@@ -183,7 +183,7 @@
         return remote(ref, ref, p_s.at[1, dx * parts + dy, jj], p_r.at[1, slot(dx, yy), jj], partner)
 
     def c_send(w, j):
-        return remote(cs.at[w, j], cr.at[w, j], c_s.at[w, j], c_r.at[w, j], dev(z, 1 - x, c, y))
+        return remote(cs.at[w, j], cr.at[w, j], c_s.at[w], c_r.at[w, j], dev(z, 1 - x, c, y))
 
     def e_send():
         return remote(eout, ein, e_s, e_r, dev(z, 1 - x, c, y))
@@ -192,14 +192,14 @@
         return remote(cout, cin, ch_s, ch_r, dev(z + 1, x, c, y))
 
     def o_send(j):
-        return remote(ost.at[j], out_ref.at[:, ds(j * blk + c * bw, bw, bw)], o_s.at[j], o_r.at[j], partner)
+        return remote(ost.at[j], out_ref.at[:, ds(j * blk + c * bw, bw, bw)], o_s, o_r, partner)
 
     def o_keep(j):
-        return pltpu.make_async_copy(omine.at[j], out_ref.at[:, ds(j * blk + c * bw, bw, bw)], o_l.at[j])
+        return pltpu.make_async_copy(omine.at[j], out_ref.at[:, ds(j * blk + c * bw, bw, bw)], o_l)
 
     def o_got(j):
         ref = out_ref.at[:, ds(j * blk + (1 - c) * bw, bw, bw)]
-        return remote(ost.at[j], ref, o_s.at[j], o_r.at[j], partner)
+        return remote(ost.at[j], ref, o_s, o_r, partner)
 
     def each(n, f):
         def body(i, carry):
@@ -334,8 +334,7 @@
 
     each(chunks, first_sends)
 
-    for t in range(5):
-        each(chunks, lambda j: raw_local(t, j).wait())
+    pltpu.make_async_copy(raw, raw, l_raw).wait()
     for e in range(sub):
         band = slice(e * LANES, (e + 1) * LANES)
         rate, theta, scale, o_re, o_im = (raw[t, :, band] for t in range(5))
@@ -365,11 +364,10 @@
 
     span_of()
 
-    def te_ready(j):
-        te_local(j).wait()
-        te_swap(j).wait_recv()
-
-    each(chunks, te_ready)
+    te_mine = te.at[ds(c * rows, rows, rows), :]
+    te_theirs = te.at[ds((1 - c) * rows, rows, rows), :]
+    pltpu.make_async_copy(te_mine, te_mine, l_te).wait()
+    remote(te_theirs, te_theirs, te_s, te_r, partner).wait_recv()
 
     def lay(i, carry):
         for e in range(sub):
@@ -711,39 +709,43 @@
 
     each(chunks - 1, last)
     finish(chunks - 1)
-    each(chunks, lambda j: o_keep(j).wait())
-    each(chunks, lambda j: o_got(j).wait_recv())
-
-    def settle(j):
-        for w in range(2):
-            w_swap(w, j).wait_send()
-            for side in range(2):
-                @pl.when(wanted(w, j, side))
-                def _():
-                    z_send(w, j, z, side).wait_send()
-            for d in range(1, lines - 1):
-                for o, side, there in ((z - d, 1, z - d >= 0), (z + d, 0, z + d < lines)):
-                    @pl.when(is_mid & there & wanted(w, j, side))
+    pltpu.make_async_copy(omine, omine, o_l).wait()
+    remote(ost, ost, o_s, o_r, partner).wait_recv()
+
+    def sent(ref, sem):
+        remote(ref, ref, sem, o_r, partner).wait_send()
+
+    for w in range(2):
+        sent(W.at[w, :, ds(z * blk + c * bw, bw, bw)], sw_s.at[w])
+        for k in range(lines):
+            for side, first, count in ((0, k, lines - k), (1, 0, k + 1)):
+                target = k + (1 if side else -1)
+                if 0 <= target < lines:
+                    n = kept if w == 0 and target in (0, lines - 1) else chunks
+
+                    if k in (0, lines - 1):
+                        first, count = k, 1
+
+                    @pl.when(z == k)
                     def _():
-                        z_send(w, j, o, side).wait_send()
-        te_swap(j).wait_send()
-        o_send(j).wait_send()
-        c_send(1, j).wait_send()
-
-        @pl.when(is_mid | (j < kept))
-        def _():
-            c_send(0, j).wait_send()
-
-        @pl.when(is_host & (j >= kept))
-        def _():
-            c_send(2, j).wait_send()
-            back_send(j).wait_send()
-
-        @pl.when(is_end)
-        def _():
-            g_send(j).wait_send()
-
-    each(chunks, settle)
+                        sent(W.at[w, pl.ds(0, n), pl.ds(first * blk, count * blk)], z_s.at[side, w])
+    sent(te_mine, te_s)
+    sent(ost, o_s)
+    sent(cs.at[1], c_s.at[1])
+
+    @pl.when(is_mid)
+    def _():
+        sent(cs.at[0], c_s.at[0])
+
+    @pl.when(is_end)
+    def _():
+        sent(cs.at[0, pl.ds(0, kept)], c_s.at[0])
+        sent(G, g_s)
+
+    @pl.when(is_host)
+    def _():
+        sent(cs.at[2, pl.ds(kept, chunks - kept)], c_s.at[2])
+        sent(bs.at[pl.ds(kept, chunks - kept)], b_s)
 
     def settle_tokens(g):
         def go(jj):
@@ -830,31 +832,31 @@
             pltpu.VMEM((rows, width), BF16),
             pltpu.VMEM((chunks, two, bw), BF16),
             dma((2, chunks)),
-            dma((chunks,)),
+            dma,
             dma((halves,)),
-            dma((5, chunks)),
+            dma,
+            dma((2,)),
             dma((2, chunks)),
-            dma((2, chunks)),
-            dma((chunks,)),
-            dma((chunks,)),
-            dma((2, 2, chunks, lines)),
+            dma,
+            dma,
+            dma((2, 2)),
             dma((2, chunks, lines)),
             dma((4, n, halves)),
             dma((4, n, halves)),
             dma((3, n, halves)),
             dma((3, n, halves)),
+            dma,
             dma((chunks,)),
-            dma((chunks,)),
-            dma((chunks,)),
-            dma,
-            dma,
-            dma,
-            dma,
+            dma,
+            dma,
+            dma,
+            dma,
+            dma,
+            dma((3,)),
             dma((3, chunks)),
-            dma((3, chunks)),
-            dma((chunks,)),
-            dma((chunks,)),
-            dma((chunks,)),
+            dma,
+            dma,
+            dma,
         ],
         compiler_params=pltpu.CompilerParams(
             collective_id=0, has_side_effects=True, vmem_limit_bytes=56 * 1024 * 1024

time: 136 us -> 135 us (level)
  Pallas kernels: 133 us -> 131 us
where the time goes in v8:
time: 135 us; the launch traced here: 134 us
  Pallas kernels  131 us (97%)
  local copies, waits for them, and re-layouts  2.3 us (2%)
    pallas_call x1, Pallas kernels, per_device(): pl.pallas_call(functools.partial(mixer_kernel, lines, parts, dims, chunks...  131 us

profile of v8, /device:TPU:0, one launch (start us, length us, event | category | flops | bytes accessed | tf_op | source)
XLA Modules:
  0.0 133.8 jit_solution(13476657469431848840)
XLA Ops:
  0.0 131.4 %mixer.1 = bf16[256,2048]{1,0:T(8,128)(2,1)} custom-call(bf16[256,2048]{1,0:T(8,128)(2,1)} %tok.1, bf16[256,2048]{1,0:T(8,128)(2,1)} %gate_w.1, bf16[256,2048]{1,0:T(8,128)(2,1)} %out_w.1, f32[16,2048]{1,0:T(8,128)} %bitcast.6, f32[16,2048]{1,0:T(8,128)} %bitcast.7, f32[16,2048]{1,0:T(8,128)} %bitcast.8, f32[2,16,2048]{2,1,0:T(8,128)} %bitcast.5, ...), custom_call_target="tpu_custom_call" | custom-call | flops 8589934592 | bytes 2097152 | tf_op jit(solution)/shard_map/mixer/pallas_call | solution.py:806
  131.4 2.3 %copy.10 = bf16[256,2048]{1,0:T(8,128)(2,1)} copy(bf16[256,2048]{1,0:T(8,128)(2,1)} %mixer.1) | data formatting | bytes 2097152

commit v9 on v8

--- a/solution.py
+++ b/solution.py
@@ -18,8 +18,8 @@
     lines, parts, dims, kept,
     tok, gate_w, out_w, decay, angle, in_coef, out_coef, skip_in,
     out_ref,
-    raw, q_re_ref, q_im_ref, c_re_ref, c_im_ref, s_re_ref, s_im_ref, skip_ref, te, x2d, y2d, st, ein, eout, cin, cout, A, W, own, own_g, cs, cr, hid, ost, omine, G, bs,
-    l_w, l_te, l_a, l_raw, sw_s, sw_r, te_s, te_r, z_s, z_r, x_s, x_r, p_s, p_r, g_s, g_r, b_s, e_s, e_r, ch_s, ch_r, c_s, c_r, o_s, o_r, o_l,
+    raw, q_re_ref, q_im_ref, c_re_ref, c_im_ref, s_re_ref, s_im_ref, skip_ref, te, x2d, y2d, st, ein, eout, cin, cout, A, W, own, own_g, cs, cr, hid, ost, G, bs,
+    l_w, l_te, l_a, l_raw, sw_s, sw_r, te_s, te_r, z_s, z_r, x_s, x_r, p_s, p_r, g_s, g_r, b_s, e_s, e_r, ch_s, ch_r, c_s, c_r, o_s, o_r,
 ):
     rows, width = tok.shape
     bw = gate_w.shape[0]
@@ -193,13 +193,6 @@
 
     def o_send(j):
         return remote(ost.at[j], out_ref.at[:, ds(j * blk + c * bw, bw, bw)], o_s, o_r, partner)
-
-    def o_keep(j):
-        return pltpu.make_async_copy(omine.at[j], out_ref.at[:, ds(j * blk + c * bw, bw, bw)], o_l)
-
-    def o_got(j):
-        ref = out_ref.at[:, ds(j * blk + (1 - c) * bw, bw, bw)]
-        return remote(ost.at[j], ref, o_s, o_r, partner)
 
     def each(n, f):
         def body(i, carry):
@@ -688,8 +681,7 @@
         theirs = ds((1 - c) * rows, rows, rows)
         ost[j] = (own[j, theirs, :] + cr[1, j, theirs, :].astype(F32)).astype(BF16)
         o_send(j).start()
-        omine[j] = (own[j, mine, :] + cr[1, j, mine, :].astype(F32)).astype(BF16)
-        o_keep(j).start()
+        out_ref[:, ds(j * blk + c * bw, bw, bw)] = (own[j, mine, :] + cr[1, j, mine, :].astype(F32)).astype(BF16)
 
     def mix(j):
         @pl.when(halves + j < chunks)
@@ -709,7 +701,6 @@
 
     each(chunks - 1, last)
     finish(chunks - 1)
-    pltpu.make_async_copy(omine, omine, o_l).wait()
     remote(ost, ost, o_s, o_r, partner).wait_recv()
 
     def sent(ref, sem):
@@ -806,8 +797,8 @@
     return pl.pallas_call(
         functools.partial(mixer_kernel, lines, parts, dims, chunks - max(1, chunks * GUESTS // 4)),
         in_specs=[hbm] * 7 + [vmem],
-        out_specs=hbm,
-        out_shape=jax.ShapeDtypeStruct((rows, width), BF16),
+        out_specs=vmem,
+        out_shape=pltpu.VMEM((rows, width), BF16),
         scratch_shapes=[
             pltpu.VMEM((5, dims, chunks * bw), F32),
         ] + [pltpu.VMEM((dims * sub, LANES), F32)] * 6 + [
@@ -828,7 +819,6 @@
             pltpu.VMEM((3, chunks, two, bw), BF16),
             pltpu.VMEM((chunks, two, bw), BF16),
             pltpu.VMEM((chunks, rows, bw), BF16),
-            pltpu.VMEM((chunks, rows, bw), BF16),
             pltpu.VMEM((rows, width), BF16),
             pltpu.VMEM((chunks, two, bw), BF16),
             dma((2, chunks)),
@@ -854,7 +844,6 @@
             dma,
             dma((3,)),
             dma((3, chunks)),
-            dma,
             dma,
             dma,
         ],

time: 135 us -> 134 us (level)
  no operation moved by 1% of the time
where the time goes in v9:
time: 134 us; the launch traced here: 132 us
  Pallas kernels  131 us (98%)
    pallas_call x1, Pallas kernels, per_device(): pl.pallas_call(functools.partial(mixer_kernel, lines, parts, dims, chunks...  131 us

profile of v9, /device:TPU:0, one launch (start us, length us, event | category | flops | bytes accessed | tf_op | source)
XLA Modules:
  0.0 132.3 jit_solution(4317553033273441237)
XLA Ops:
  0.0 131.3 %mixer.1 = bf16[256,2048]{1,0:T(8,128)(2,1)S(1)} custom-call(bf16[256,2048]{1,0:T(8,128)(2,1)} %tok.1, bf16[256,2048]{1,0:T(8,128)(2,1)} %gate_w.1, bf16[256,2048]{1,0:T(8,128)(2,1)} %out_w.1, f32[16,2048]{1,0:T(8,128)} %bitcast.6, f32[16,2048]{1,0:T(8,128)} %bitcast.7, f32[16,2048]{1,0:T(8,128)} %bitcast.8, f32[2,16,2048]{2,1,0:T(8,128)} %bitcast.5, ...), custom_call_target="tpu_custom_call" | custom-call | flops 8589934592 | bytes 2097152 | tf_op jit(solution)/shard_map/mixer/pallas_call | solution.py:797
  131.3 1.0 copy.10

commit v10 on v9

--- a/solution.py
+++ b/solution.py
@@ -683,15 +683,37 @@
         o_send(j).start()
         out_ref[:, ds(j * blk + c * bw, bw, bw)] = (own[j, mine, :] + cr[1, j, mine, :].astype(F32)).astype(BF16)
 
+    def end_mix(j, near, far):
+        for o in range(lines):
+            if o != far and o != lines - 1 - far:
+                z_send(1, j, o, 0).wait_recv()
+        mine = ds(x * two, two, two)
+        other = ds((1 - x) * two, two, two)
+        last_cols = pl.ds(far * blk, blk)
+        own_g[j] = jnp.dot(A[1, other, near], W[1, j, near], preferred_element_type=F32)
+        own[j] = jnp.dot(A[1, mine, near], W[1, j, near], preferred_element_type=F32)
+        z_send(1, j, far, 0).wait_recv()
+        right = W[1, j, last_cols]
+        cs[1, j] = (own_g[j] + jnp.dot(A[1, other, last_cols], right, preferred_element_type=F32)).astype(BF16)
+        c_send(1, j).start()
+        own[j] += jnp.dot(A[1, mine, last_cols], right, preferred_element_type=F32)
+
     def mix(j):
         @pl.when(halves + j < chunks)
         def _():
             forward_far(1, halves + j)
 
-        @pl.when(is_end)
-        def _():
-            at_end(1, j)
-        multiply(1, 1, 1, j, own)
+        @pl.when(is_mid)
+        def _():
+            multiply(1, 1, 1, j, own)
+
+        @pl.when(z == 0)
+        def _():
+            end_mix(j, pl.ds(0, (lines - 1) * blk), lines - 1)
+
+        @pl.when(z == lines - 1)
+        def _():
+            end_mix(j, pl.ds(blk, (lines - 1) * blk), 0)
 
     mix(0)
 

time: 134 us -> 133 us (level)
  no operation moved by 1% of the time
where the time goes in v10:
time: 133 us; the launch traced here: 131 us
  Pallas kernels  130 us (98%)
    pallas_call x1, Pallas kernels, per_device(): pl.pallas_call(functools.partial(mixer_kernel, lines, parts, dims, chunks...  130 us

profile of v10, /device:TPU:0, one launch (start us, length us, event | category | flops | bytes accessed | tf_op | source)
XLA Modules:
  0.0 131.5 jit_solution(17310440068236449946)
XLA Ops:
  0.0 130.5 %mixer.1 = bf16[256,2048]{1,0:T(8,128)(2,1)S(1)} custom-call(bf16[256,2048]{1,0:T(8,128)(2,1)} %tok.1, bf16[256,2048]{1,0:T(8,128)(2,1)} %gate_w.1, bf16[256,2048]{1,0:T(8,128)(2,1)} %out_w.1, f32[16,2048]{1,0:T(8,128)} %bitcast.6, f32[16,2048]{1,0:T(8,128)} %bitcast.7, f32[16,2048]{1,0:T(8,128)} %bitcast.8, f32[2,16,2048]{2,1,0:T(8,128)} %bitcast.5, ...), custom_call_target="tpu_custom_call" | custom-call | flops 8589934592 | bytes 2097152 | tf_op jit(solution)/shard_map/mixer/pallas_call | solution.py:819
  130.5 1.0 copy.10
